TPU v7x, 128 devices: a whole 4x4x4 slice. The times are simulated.
128 devices in a mesh: seq: 16 (over y, x), head: 8 (over z, core).
Axes of the slice: x: 4, y: 4, z: 4, core: 2. Of those that a mesh axis runs over, the one named last changes fastest.
Arguments:
- segment_input: bfloat16 [2, 4096, 3584], P(None, 'seq'), may hold values from -16 to 16
- doc_ids: int32 [2, 4096], replicated, may hold values from 0 to 3, never falling along the last dimension, each value on 1 to 2048 neighbouring positions
- memory: bfloat16 [32, 3584], replicated, may hold values from -16 to 16
- gain: bfloat16 [3584], replicated, may hold values from 0.099609375 to 1.8984375
- w_query: bfloat16 [3584, 4096], P(None, 'head'), may hold values from -4 to 4
- w_key: bfloat16 [3584, 2048], P(None, 'head'), may hold values from -4 to 4
- w_value: bfloat16 [3584, 2048], P(None, 'head'), may hold values from -0.09375 to 0.09375
- w_out: bfloat16 [4096, 3584], P(None, 'head'), may hold values from -0.09375 to 0.09375
- mem_proj: bfloat16 [3584, 3584], P('head'), may hold values from -4 to 4
Outputs:
- hidden: bfloat16 [2, 4096, 3584], P(None, 'seq', 'head')
- new_memory: bfloat16 [32, 3584], replicated
Inputs may be any that keep to these rules, and one draw needn't show every extreme that they name: `doc_ids`: ids never fall along a segment; each document has 1 to 2048 tokens.
All inputs are finite; a program needn't handle non-finite values.
Results may differ from a plain program's by a relative error of at most 0.02.
Values may be sent and summed in bfloat16 or wider, within the bound.
No kernel may reach another device: no remote copies, remote signals or barrier semaphores. Data moves between devices by JAX's collectives and lax.ppermute only.
A program may use at most 128 MiB of HBM per device.

v0:
```python
import functools
import math

import jax
import jax.numpy as jnp
from jax import lax
from jax.experimental import pallas as pl
from jax.experimental.pallas import tpu as pltpu
from jax.sharding import PartitionSpec as P


D = 3584
HD = 256
M = 32
ROWS = 256
COLS = 448
HALF = D // 2
KC = 512
SHAPE = 4
LOG2E_SCALE = math.log2(math.e) / 16.0
LOW = -1e30
BF = jnp.bfloat16
F32 = jnp.float32


WHOLE = pl.BlockSpec(memory_space=pltpu.VMEM)


def params(mib, **kw):
    return pltpu.CompilerParams(vmem_limit_bytes=mib * 1024 * 1024, **kw)


def dot(a, b):
    return jnp.dot(a, b, preferred_element_type=F32)


def dot_t(a, b):
    return lax.dot_general(a, b, (((1,), (1,)), ((), ())), preferred_element_type=F32)


def normed(rows, gain):
    v = rows.astype(F32)
    r = lax.rsqrt(jnp.mean(v * v, axis=-1, keepdims=True) + 1e-6)
    return (v * r * gain.astype(F32)).astype(BF)


def column(row):
    return jnp.broadcast_to(row, (128, row.shape[1])).T[:, :1]


def as_row(col):
    return jnp.broadcast_to(col, (col.shape[0], 128)).T[:1, :]


def attend(score_list, value_list):
    peak = functools.reduce(jnp.maximum, [jnp.max(s, axis=1, keepdims=True) for s in score_list])
    peak = jnp.maximum(peak, -1e29)
    total = 0.0
    mixed = 0.0
    for s, v in zip(score_list, value_list):
        p = jnp.exp2(s - peak)
        total = total + jnp.sum(p, axis=1, keepdims=True)
        mixed = mixed + dot(p.astype(BF), v)
    some = total > 0.0
    out = mixed / jnp.where(some, total, 1.0)
    return out, jnp.where(some, peak + jnp.log2(jnp.where(some, total, 1.0)), LOW)


def memory_part(qkvm, key_blocks, first, out_ref):
    for g in range(2):
        q = qkvm[:, g * HD : (g + 1) * HD]
        scores = [dot_t(q, kv[:, :HD]) * LOG2E_SCALE for kv in key_blocks]
        sm = dot_t(q, qkvm[:, 2 * HD : 3 * HD]) * LOG2E_SCALE
        scores.append(jnp.where(first, sm, LOW))
        out, lse = attend(scores, [kv[:, HD:] for kv in key_blocks] + [qkvm[:, 3 * HD :]])
        hi = lse.astype(BF)
        lo = (lse - hi.astype(F32)).astype(BF)
        lane = lax.broadcasted_iota(jnp.int32, (M, 128), 1)
        stats = jnp.where(lane == 0, hi.astype(F32), jnp.where(lane == 1, lo.astype(F32), 0.0))
        out_ref[g * M : (g + 1) * M, :HD] = out.astype(BF)
        out_ref[g * M : (g + 1) * M, HD:] = stats.astype(BF)


def place():
    i = lax.axis_index("seq")
    h = lax.axis_index("head")
    return i % SHAPE, i // SHAPE, h // 2, h % 2


def scaled_chunk(x, gain, squares, rows, first):
    v = x.astype(F32)
    sq = v * v
    part = sq[:, :128]
    for n in range(1, KC // 128):
        part = part + sq[:, n * 128 : (n + 1) * 128]
    squares[rows, :] = part if first else squares[rows, :] + part
    return (v * gain).astype(BF)


def norm_of(squares):
    return lax.rsqrt(jnp.sum(squares[...], axis=1, keepdims=True) / D + 1e-6)


def accumulate(acc, a, ws, first):
    at = 0
    for w in ws:
        span = slice(at, at + w.shape[1])
        part = dot(a, w)
        acc[:, span] = part if first else acc[:, span] + part
        at = at + w.shape[1]


def first_kernel(x, mem, gain, wq, wk, wv, q_ref, kv_ref, qkvm_ref, part_ref, *refs):
    bufs, (xs, ms, squares, acc, sems) = refs[:3], refs[3:]
    groups = []
    for k in range(D // KC):
        span = pl.ds(k * KC, KC)
        pairs = [(x.at[0, :, span], xs.at[:, span]), (mem.at[:, span], ms.at[:, span])]
        pairs += [(w.at[span, :], buf.at[span, :]) for w, buf in zip((wq, wk, wv), bufs)]
        groups.append(
            [pltpu.make_async_copy(p, q, sems.at[k, n]) for n, (p, q) in enumerate(pairs)]
        )
    for group in groups:
        for c in group:
            c.start()
    g = gain[...].astype(F32).reshape(1, D)
    for k, group in enumerate(groups):
        for c in group:
            c.wait()
        span = slice(k * KC, (k + 1) * KC)
        top = scaled_chunk(xs[:, span], g[:, span], squares, slice(0, ROWS), k == 0)
        low = scaled_chunk(ms[:, span], g[:, span], squares, slice(ROWS, ROWS + M), k == 0)
        a = jnp.concatenate([top, low], axis=0)
        accumulate(acc, a, [buf[span, :] for buf in bufs], k == 0)
    out = (acc[...] * norm_of(squares)).astype(BF)
    q_ref[...] = out[:ROWS, : 2 * HD]
    kv_ref[...] = out[:ROWS, 2 * HD :]
    qkvm_ref[...] = out[ROWS:, :]
    px, py, _, _ = place()
    memory_part(qkvm_ref[...], [kv_ref[...]], px + py == 0, part_ref)


def first_project(x, mem, gain, wq, wk, wv):
    hbm = pl.BlockSpec(memory_space=pltpu.HBM)
    shapes = [(ROWS, 2 * HD), (ROWS, 2 * HD), (M, 4 * HD), (2 * M, HD + 128)]
    shapes += [wq.shape, wk.shape, wv.shape]
    return pl.pallas_call(
        first_kernel,
        in_specs=[hbm, hbm, WHOLE, hbm, hbm, hbm],
        out_specs=[WHOLE] * len(shapes),
        out_shape=[jax.ShapeDtypeStruct(s, BF) for s in shapes],
        scratch_shapes=[
            pltpu.VMEM((ROWS, D), BF),
            pltpu.VMEM((M, D), BF),
            pltpu.VMEM((ROWS + M, 128), F32),
            pltpu.VMEM((ROWS + M, 4 * HD), F32),
            pltpu.SemaphoreType.DMA((D // KC, 5)),
        ],
        compiler_params=params(28),
        cost_estimate=pl.CostEstimate(
            flops=2 * (ROWS + M) * D * 4 * HD, bytes_accessed=10 * 2**20, transcendentals=512
        ),
        name="first_project",
    )(x, mem, gain, wq, wk, wv)


def window(h):
    return pl.multiple_of((h * 7 // 2) * 128, 128)


def second_kernel(x, gain, wq, wk, wv, q0, wt, proj, *refs):
    q_ref, kv_ref, wt_buf, proj_buf, cols_buf, xs, squares, acc, sems, wsems = refs
    _, _, z, c = place()
    copies = []
    for k in range(D // KC):
        span = pl.ds(k * KC, KC)
        copies.append(pltpu.make_async_copy(x.at[1, :, span], xs.at[:, span], sems.at[k]))
    late = [
        pltpu.make_async_copy(src, dst, wsems.at[n])
        for n, (src, dst) in enumerate(
            (
                (wt, wt_buf),
                (proj, proj_buf),
                (x.at[:, :, pl.ds(window(2 * z + c), 512)], cols_buf),
            )
        )
    ]
    for c in copies + late:
        c.start()
    q_ref[0] = q0[...]
    g = gain[...].astype(F32).reshape(1, D)
    for k, c in enumerate(copies):
        c.wait()
        span = slice(k * KC, (k + 1) * KC)
        a = scaled_chunk(xs[:, span], g[:, span], squares, slice(0, ROWS), k == 0)
        accumulate(acc, a, [w[span, :] for w in (wq, wk, wv)], k == 0)
    out = (acc[...] * norm_of(squares)).astype(BF)
    q_ref[1] = out[:, : 2 * HD]
    kv_ref[...] = out[:, 2 * HD :]
    for c in late:
        c.wait()


def second_project(x, gain, wq, wk, wv, q0, wt, proj):
    hbm = pl.BlockSpec(memory_space=pltpu.HBM)
    shapes = [(2, ROWS, 2 * HD), (ROWS, 2 * HD), wt.shape, proj.shape, (2, ROWS, 512)]
    return pl.pallas_call(
        second_kernel,
        in_specs=[hbm] + [WHOLE] * 5 + [hbm, hbm],
        out_specs=[WHOLE] * len(shapes),
        out_shape=[jax.ShapeDtypeStruct(s, BF) for s in shapes],
        scratch_shapes=[
            pltpu.VMEM((ROWS, D), BF),
            pltpu.VMEM((ROWS, 128), F32),
            pltpu.VMEM((ROWS, 4 * HD), F32),
            pltpu.SemaphoreType.DMA((D // KC,)),
            pltpu.SemaphoreType.DMA((3,)),
        ],
        compiler_params=params(28),
        cost_estimate=pl.CostEstimate(
            flops=2 * ROWS * D * 4 * HD, bytes_accessed=10 * 2**20, transcendentals=512
        ),
        name="second_project",
    )(x, gain, wq, wk, wv, q0, wt, proj)


def memory_project_kernel(own, other, gain, wq, wk, wv, *refs):
    kvs, (qkvm_ref, part_ref, whole_ref) = refs[:4], refs[4:]
    px, _, _, c = place()
    whole_ref[:, pl.ds(pl.multiple_of(c * HALF, 128), HALF)] = own[...]
    whole_ref[:, pl.ds(pl.multiple_of((1 - c) * HALF, 128), HALF)] = other[...]
    a = normed(whole_ref[...], gain[...].reshape(1, D))
    qkvm_ref[:, : 2 * HD] = dot(a, wq[...]).astype(BF)
    qkvm_ref[:, 2 * HD : 3 * HD] = dot(a, wk[...]).astype(BF)
    qkvm_ref[:, 3 * HD :] = dot(a, wv[...]).astype(BF)
    memory_part(qkvm_ref[...], [kv[...] for kv in kvs], px == 0, part_ref)


def memory_project(own, other, gain, wq, wk, wv, kvs):
    return pl.pallas_call(
        memory_project_kernel,
        in_specs=[WHOLE] * 10,
        out_specs=[WHOLE] * 3,
        out_shape=[
            jax.ShapeDtypeStruct((M, 4 * HD), BF),
            jax.ShapeDtypeStruct((2 * M, HD + 128), BF),
            jax.ShapeDtypeStruct((M, D), BF),
        ],
        compiler_params=params(20),
        cost_estimate=pl.CostEstimate(
            flops=2 * 256 * D * 4 * HD, bytes_accessed=8 * 1024 * 1024, transcendentals=M
        ),
        name="memory_project",
    )(own, other, gain, wq, wk, wv, *kvs)


def memory_combine_kernel(last, a, b, out_ref):
    parts = [r[...].astype(F32) for r in (a, b)]
    lses = [p[:, HD : HD + 1] + p[:, HD + 1 : HD + 2] for p in parts]
    peak = functools.reduce(jnp.maximum, lses)
    ws = [jnp.exp2(s - peak) for s in lses]
    total = sum(ws)
    out = sum(w * p[:, :HD] for w, p in zip(ws, parts)) / total
    if last:
        out_ref[:, :HD] = out[:M].astype(BF)
        out_ref[:, HD:] = out[M:].astype(BF)
    else:
        lse = peak + jnp.log2(total)
        hi = lse.astype(BF).astype(F32)
        lane = lax.broadcasted_iota(jnp.int32, (2 * M, 128), 1)
        stats = jnp.where(lane == 0, hi, jnp.where(lane == 1, lse - hi, 0.0))
        out_ref[:, :HD] = out.astype(BF)
        out_ref[:, HD:] = stats.astype(BF)


def memory_combine(a, b, last=False):
    shape = (M, 2 * HD) if last else (2 * M, HD + 128)
    return pl.pallas_call(
        functools.partial(memory_combine_kernel, last),
        in_specs=[WHOLE] * 2,
        out_specs=WHOLE,
        out_shape=jax.ShapeDtypeStruct(shape, BF),
        compiler_params=params(4),
        cost_estimate=pl.CostEstimate(flops=10**8, bytes_accessed=10**5, transcendentals=256),
        name="memory_combine",
    )(a, b)


def memory_write_kernel(blocks, mem, w_out, proj, keep_ref, send_ref):
    _, _, z, c = place()
    wide = mem[:, pl.ds(window(2 * z + c), 512)].astype(F32)
    acc = jnp.where(c == 1, wide[:, 64:], wide[:, :COLS])
    far = SHAPE - 1 - z
    for k, zz in enumerate((z, flip(z), far, flip(far))):
        for e in range(2):
            h = zz * 2 + (c if e == 0 else 1 - c)
            w = w_out[:, pl.ds(pl.multiple_of(h * 2 * HD, 2 * HD), 2 * HD)]
            acc = acc + dot_t(blocks[2 * k + e], w)
    a = acc.astype(BF)
    keep_ref[...] = dot(a, proj[:, pl.ds(pl.multiple_of(c * HALF, 128), HALF)]).astype(BF)
    send_ref[...] = dot(a, proj[:, pl.ds(pl.multiple_of((1 - c) * HALF, 128), HALF)]).astype(BF)


def finish_kernel(own, other, out_ref):
    _, _, _, c = place()
    out_ref[:, pl.ds(pl.multiple_of(c * HALF, 128), HALF)] = own[...]
    out_ref[:, pl.ds(pl.multiple_of((1 - c) * HALF, 128), HALF)] = other[...]


def finish(own, other):
    return pl.pallas_call(
        finish_kernel,
        in_specs=[WHOLE] * 2,
        out_specs=WHOLE,
        out_shape=jax.ShapeDtypeStruct((M, D), BF),
        compiler_params=params(4),
        name="finish",
    )(own, other)


def flip(i):
    return i + 1 - 2 * lax.rem(i, 2)


def memory_write(blocks, mem, w_out, proj):
    return pl.pallas_call(
        memory_write_kernel,
        in_specs=[WHOLE] * 4,
        out_specs=[WHOLE] * 2,
        out_shape=[jax.ShapeDtypeStruct((M, HALF), BF)] * 2,
        compiler_params=params(20),
        cost_estimate=pl.CostEstimate(
            flops=2 * 256 * D * 8 * COLS, bytes_accessed=8 * 1024 * 1024, transcendentals=0
        ),
        name="memory_write",
    )(blocks, mem, w_out, proj)


def token_kernel(seg, docs, q0, q1, q2, q3, kva, kvb, kvc, o0, o1, o2, o3, kvs, kcode):
    x, y, _, _ = place()
    lane = lax.broadcasted_iota(jnp.int32, (1, ROWS), 1).astype(F32)
    for n, ref in enumerate((kva, kvb, kvc)):
        kvs[n * ROWS : (n + 1) * ROWS, :] = ref[...]
        block = (y - 2 + n) * SHAPE + x
        start = jnp.maximum(block, 0) * ROWS
        doc = docs[seg : seg + 1, pl.ds(pl.multiple_of(start, ROWS), ROWS)].astype(F32)
        code = doc * 4096.0 + lane + start.astype(F32)
        kcode[:, n * ROWS : (n + 1) * ROWS] = jnp.where(block >= 0, code, -1.0)
    for d, (q_ref, o_ref) in enumerate(zip((q0, q1, q2, q3), (o0, o1, o2, o3))):
        start = (y * SHAPE + lax.rem(x - d + SHAPE, SHAPE)) * ROWS
        doc = docs[seg : seg + 1, pl.ds(pl.multiple_of(start, ROWS), ROWS)].astype(F32)
        low = column(doc * 4096.0)
        high = column(doc * 4096.0 + lane + start.astype(F32))
        if d == 0:
            codes = kcode[...]
            keys = kvs[...]
        else:
            at = jnp.where(x >= d, 0, ROWS)
            at = pl.multiple_of(at, ROWS)
            codes = kcode[:, pl.ds(at, 2 * ROWS)]
            keys = kvs[pl.ds(at, 2 * ROWS), :]
        valid = (codes >= low) & (codes <= high)
        for g in range(2):
            q = q_ref[seg, :, g * HD : (g + 1) * HD]
            scores = jnp.where(valid, dot_t(q, keys[:, :HD]) * LOG2E_SCALE, LOW)
            out, lse = attend([scores], [keys[:, HD:]])
            row = as_row(lse)
            hi = row.astype(BF).astype(F32)
            sub = lax.broadcasted_iota(jnp.int32, (16, ROWS), 0)
            stats = jnp.where(sub == 0, hi, jnp.where(sub == 1, row - hi, 0.0))
            o_ref[:ROWS, g * HD : (g + 1) * HD] = out.astype(BF)
            o_ref[ROWS:, g * HD : (g + 1) * HD] = stats.astype(BF)


def token_attention(docs, seg, qs, kva, kvb, kvc):
    return pl.pallas_call(
        functools.partial(token_kernel, seg),
        in_specs=[WHOLE] * 8,
        out_specs=[WHOLE] * 4,
        out_shape=[jax.ShapeDtypeStruct((ROWS + 16, 2 * HD), BF)] * 4,
        scratch_shapes=[pltpu.VMEM((3 * ROWS, 2 * HD), BF), pltpu.VMEM((1, 3 * ROWS), F32)],
        compiler_params=params(16),
        cost_estimate=pl.CostEstimate(
            flops=3 * 10**9, bytes_accessed=4 * 10**6, transcendentals=10**6
        ),
        name="token_attention",
    )(docs, *qs, kva, kvb, kvc)


def token_combine_kernel(seg, q, qkvm, a, b, c, d, out_ref):
    refs = (a, b, c, d)
    for g in range(2):
        lanes = slice(g * HD, (g + 1) * HD)
        scores = dot_t(q[seg, :, lanes], qkvm[:, 2 * HD : 3 * HD]) * LOG2E_SCALE
        out, lse = attend([scores], [qkvm[:, 3 * HD :]])
        outs, lses = [out], [lse]
        for r in refs:
            tail = r[ROWS:, lanes].astype(F32)
            lses.append(column(tail[0:1, :] + tail[1:2, :]))
            outs.append(r[:ROWS, lanes].astype(F32))
        peak = functools.reduce(jnp.maximum, lses)
        ws = [jnp.exp2(s - peak) for s in lses]
        mixed = sum(w * o for w, o in zip(ws, outs)) / sum(ws)
        out_ref[:, lanes] = mixed.astype(BF)


def token_combine(seg, q, qkvm, parts):
    return pl.pallas_call(
        functools.partial(token_combine_kernel, seg),
        in_specs=[WHOLE] * 6,
        out_specs=WHOLE,
        out_shape=jax.ShapeDtypeStruct((ROWS, 2 * HD), BF),
        compiler_params=params(12),
        cost_estimate=pl.CostEstimate(flops=5 * 10**8, bytes_accessed=10**6, transcendentals=4096),
        name="token_combine",
    )(q, qkvm, *parts)


def token_out_kernel(seg, *refs):
    blocks, cols, w_out, out_ref, flat = refs[:8], refs[8], refs[9], refs[-2], refs[-1]
    _, _, z, c = place()
    acc = jnp.zeros((COLS, ROWS), F32)
    for n, ref in enumerate(blocks):
        k, e = n // 2, n % 2
        h = lax.rem(z - k + SHAPE, SHAPE) * 2 + (c if e == 0 else 1 - c)
        w = w_out[:, pl.ds(pl.multiple_of(h * 2 * HD, 2 * HD), 2 * HD)]
        acc = acc + dot_t(w, ref[...])
    for at in range(0, 512, 128):
        flat[at : at + 128, :] = cols[seg, :, at : at + 128].astype(F32).T
    out_ref[0] = (acc + flat[pl.ds(pl.multiple_of(c * 64, 64), COLS), :]).astype(BF)


def token_out(blocks, cols, seg, w_out, before):
    in_specs = [WHOLE] * 10
    args = [*blocks, cols, w_out]
    aliases = {}
    if before is not None:
        in_specs.append(pl.BlockSpec(memory_space=pl.ANY))
        args.append(before)
        aliases = {len(args) - 1: 0}
    return pl.pallas_call(
        functools.partial(token_out_kernel, seg),
        grid=(1,),
        in_specs=in_specs,
        out_specs=pl.BlockSpec((1, COLS, ROWS), lambda k: (seg, 0, 0)),
        out_shape=jax.ShapeDtypeStruct((2, COLS, ROWS), BF),
        input_output_aliases=aliases,
        scratch_shapes=[pltpu.VMEM((512, ROWS), F32)],
        compiler_params=params(12),
        cost_estimate=pl.CostEstimate(
            flops=2 * ROWS * 4096 * COLS, bytes_accessed=6 * 10**6, transcendentals=0
        ),
        name="token_out",
    )(*args)


N_SEQ, N_HEAD = SHAPE * SHAPE, 8


def x_shift(v, d):
    return lax.ppermute(
        v, "seq", [(i, i // SHAPE * SHAPE + (i + d) % SHAPE) for i in range(N_SEQ)]
    )


def y_shift(v, d):
    return lax.ppermute(v, "seq", [(i, (i + d * SHAPE) % N_SEQ) for i in range(N_SEQ)])


def y_later(v, d):
    return lax.ppermute(v, "seq", [(i, i + d * SHAPE) for i in range(N_SEQ - d * SHAPE)])


def x_near(v):
    return lax.ppermute(v, "seq", [(i, i ^ 1) for i in range(N_SEQ)])


def x_far(v):
    return lax.ppermute(v, "seq", [(i, i ^ 3) for i in range(N_SEQ)])


def y_near(v):
    return lax.ppermute(v, "seq", [(i, i ^ 4) for i in range(N_SEQ)])


def y_far(v):
    return lax.ppermute(v, "seq", [(i, i ^ 12) for i in range(N_SEQ)])


def z_near(v):
    return lax.ppermute(v, "head", [(i, i ^ 2) for i in range(N_HEAD)])


def z_far(v):
    return lax.ppermute(v, "head", [(i, i ^ 6) for i in range(N_HEAD)])


def z_shift(v, d):
    return lax.ppermute(v, "head", [(i, (i + 2 * d) % N_HEAD) for i in range(N_HEAD)])


def other_core(v):
    return lax.ppermute(v, "head", [(i, i ^ 1) for i in range(N_HEAD)])


def add(a, b):
    return (a.astype(F32) + b.astype(F32)).astype(BF)


def memory_tail(attn, mem, w_out, proj):
    pair = jnp.stack([attn, other_core(attn)])
    four = jnp.concatenate([pair, z_near(pair)])
    blocks = jnp.concatenate([four, z_far(four)])
    keep, send = memory_write(blocks, mem, w_out, proj)
    half = add(keep, other_core(send))
    half = add(half, z_near(half))
    half = add(half, z_far(half))
    return half, other_core(half)


def per_device(segment_input, doc_ids, memory, gain, w_query, w_key, w_value, w_out, mem_proj):
    in_hbm = lambda v: pltpu.with_memory_space_constraint(v, pltpu.HBM)
    x = in_hbm(segment_input)

    q0, kv0, qkvm0, part, *weights = first_project(
        x, in_hbm(memory), gain, *[in_hbm(w) for w in (w_query, w_key, w_value)]
    )
    weights = (gain, *weights)
    q, kv1, w_out, mem_proj, cols = second_project(
        x, *weights, q0, in_hbm(w_out.T), in_hbm(mem_proj)
    )

    part = memory_combine(part, x_near(part))
    part = memory_combine(part, x_far(part))
    part = memory_combine(part, y_near(part))
    attn = memory_combine(part, y_far(part), True)
    own, other = memory_tail(attn, memory, w_out, mem_proj)

    kvs0 = [kv0] + [y_later(kv0, d) for d in (1, 2)]
    kvs1 = [kv1] + [y_shift(kv1, d) for d in (1, 2, 3)]
    qkvm1, part, mem1 = memory_project(own, other, *weights, kvs1)
    part = memory_combine(part, x_near(part))
    attn = memory_combine(part, x_far(part), True)
    own, other = memory_tail(attn, mem1, w_out, mem_proj)

    hidden = None
    qs = [q] + [x_shift(q, d) for d in (1, 2, 3)]
    for s, (kvs, qkvm) in enumerate(((kvs0, qkvm0), (kvs1, qkvm1))):
        parts = token_attention(doc_ids, s, qs, kvs[2], kvs[1], kvs[0])
        parts = [parts[0]] + [x_shift(parts[d], SHAPE - d) for d in (1, 2, 3)]
        attn = token_combine(s, q, qkvm, parts)
        blocks = []
        for d in range(SHAPE):
            piece = attn if d == 0 else z_shift(attn, d)
            blocks += [piece, other_core(piece)]
        hidden = token_out(blocks, cols, s, w_out, hidden)

    return hidden.transpose(0, 2, 1), finish(own, other)


def solution(mesh):
    return jax.shard_map(
        per_device,
        mesh=mesh,
        in_specs=(
            P(None, "seq", None),
            P(),
            P(),
            P(),
            P(None, "head"),
            P(None, "head"),
            P(None, "head"),
            P(None, "head"),
            P("head", None),
        ),
        out_specs=(P(None, "seq", "head"), P()),
        check_vma=False,
    )
```

profile of v0, /device:TPU:1, one launch (start us, length us, event | category | flops | bytes accessed | tf_op | source)
XLA Modules:
  0.0 165.7 jit_solution(10833557294537710250)
XLA Ops:
  1.3 5.1 %first_project.1 = (bf16[256,512]{1,0:T(8,128)(2,1)S(1)}, bf16[256,512]{1,0:T(8,128)(2,1)S(1)}, bf16[32,1024]{1,0:T(8,128)(2,1)S(1)}, bf16[64,384]{1,0:T(8,128)(...) custom-call(bf16[2,256,3584]{2,1,0:T(8,128)(2,1)} %x.3, ...), custom_call_target="tpu_custom_call" | custom-call | flops 2113929216 | bytes 10485760 | tf_op jit(solution)/shard_map/first_project/pallas_call | solution.py:147
  10.2 2.8 %collective-permute-start.1 = (bf16[64,384]{1,0:T(8,128)(2,1)S(1)}, bf16[64,384]{1,0:T(8,128)(2,1)S(1)}, u32[]{:S(2)}, u32[]{:S(2)}) collective-permute-start(bf16[64,384]{1,0:T(8,128)(2,1)S(1)} %memory_combine.6.a), channel_id=1, source_target_pairs={{0,24},{8,16},{16,8},{24,0},{32,56},{40,48},{48,40},{56,32},{64,88... | collective-permute-start | bytes 147464 | tf_op jit(solution)/shard_map/ppermute | solution.py:479
  17.9 3.0 %collective-permute-start.3 = (bf16[64,384]{1,0:T(8,128)(2,1)S(1)}, bf16[64,384]{1,0:T(8,128)(2,1)S(1)}, u32[]{:S(2)}, u32[]{:S(2)}) collective-permute-start(bf16[64,384]{1,0:T(8,128)(2,1)S(1)} %memory_combine.8.a), channel_id=1, source_target_pairs={{0,96},{8,104},{16,112},{24,120},{32,64},{40,72},{48,80},{56,88},{... | collective-permute-start | bytes 147464 | tf_op jit(solution)/shard_map/ppermute | solution.py:487
  22.6 5.2 %collective-permute-start.4 = (bf16[32,512]{1,0:T(8,128)(2,1)S(1)}, bf16[32,512]{1,0:T(8,128)(2,1)S(1)}, u32[]{:S(2)}, u32[]{:S(2)}) collective-permute-start(bf16[32,512]{1,0:T(8,128)(2,1)S(1)} %memory_combine.9), channel_id=1, source_target_pairs={{0,1},{1,0},{2,3},{3,2},{4,5},{5,4},{6,7},{7,6},{8,9},{9,8},{10,11... | collective-permute-start | bytes 98312 | tf_op jit(solution)/shard_map/ppermute | solution.py:503
  32.5 3.2 %collective-permute-start.6 = (bf16[4,32,512]{2,1,0:T(8,128)(2,1)S(1)}, bf16[4,32,512]{2,1,0:T(8,128)(2,1)S(1)}, u32[]{:S(2)}, u32[]{:S(2)}) collective-permute-start(bf16[4,32,512]{2,1,0:T(8,128)(2,1)S(1)} %pad_maximum_fusion.2), channel_id=1, source_target_pairs={{0,6},{1,7},{2,4},{3,5},{4,2},{5,3},{6,0},{7,1},{8,14},{9,15},{10,... | collective-permute-start | bytes 393224 | tf_op jit(solution)/shard_map/ppermute | solution.py:495
  35.7 4.8 %second_project.1 = (bf16[2,256,512]{2,1,0:T(8,128)(2,1)S(1)}, bf16[256,512]{1,0:T(8,128)(2,1)S(1)}, bf16[448,4096]{1,0:T(8,128)(2,1)S(1)}, bf16[448,3584]{1,0:T(8,128)(2,1)S(1)}, bf16[2,256,512]{2,1,0:T(8,128)(2,1)S(1)}) custom-call(bf16[2,256,3584]{2,1,0:T(8,128)(2,1)} %x.3, bf16[3584]{0:T(1024)(128)(2,1)S(1)} %copy-done.1, ...), custom_call_target="tpu_custom_call" | custom-call | flops 1879048192 | bytes 10485760 | tf_op jit(solution)/shard_map/second_project/pallas_call | solution.py:207
  45.5 4.3 %collective-permute-done.8 = bf16[32,1792]{1,0:T(8,128)(2,1)S(1)} collective-permute-done((bf16[32,1792]{1,0:T(8,128)(2,1)S(1)}, bf16[32,1792]{1,0:T(8,128)(2,1)S(1)}, u32[]{:S(2)}, u32[]{:S(2)}) %collective-permute-start.8) | collective-permute-done | bytes 114720 | tf_op jit(solution)/shard_map/ppermute | solution.py:491
  51.1 3.8 %collective-permute-start.12 = (bf16[256,512]{1,0:T(8,128)(2,1)S(1)}, bf16[256,512]{1,0:T(8,128)(2,1)S(1)}, u32[]{:S(2)}, u32[]{:S(2)}) collective-permute-start(bf16[256,512]{1,0:T(8,128)(2,1)S(1)} %get-tuple-element.39.refs_0_.kvc), channel_id=1, source_target_pairs={{0,64},{8,72},{16,80},{24,88},{32,96},{40,104},{48,112},{56,120},{... | collective-permute-start | bytes 786440 | tf_op jit(solution)/shard_map/ppermute | solution.py:467
  61.0 4.5 %collective-permute-done.12.refs_2_.kva = bf16[256,512]{1,0:T(8,128)(2,1)S(1)} collective-permute-done((bf16[256,512]{1,0:T(8,128)(2,1)S(1)}, bf16[256,512]{1,0:T(8,128)(2,1)S(1)}, u32[]{:S(2)}, u32[]{:S(2)}) %collective-permute-start.12) | collective-permute-done | bytes 262176 | tf_op jit(solution)/shard_map/ppermute | solution.py:467
  65.4 2.5 %collective-permute-start.16 = (bf16[2,256,512]{2,1,0:T(8,128)(2,1)S(1)}, bf16[2,256,512]{2,1,0:T(8,128)(2,1)S(1)}, u32[]{:S(2)}, u32[]{:S(2)}) collective-permute-start(bf16[2,256,512]{2,1,0:T(8,128)(2,1)S(1)} %get-tuple-element.33.q0.q), channel_id=1, source_target_pairs={{0,24},{8,0},{16,8},{24,16},{32,56},{40,32},{48,40},{56,48},{64,88... | collective-permute-start | bytes 1572872 | tf_op jit(solution)/shard_map/ppermute | solution.py:461
  70.5 12.5 %collective-permute-done.39.b = bf16[64,384]{1,0:T(8,128)(2,1)S(1)} collective-permute-done((bf16[64,384]{1,0:T(8,128)(2,1)S(1)}, bf16[64,384]{1,0:T(8,128)(2,1)S(1)}, u32[]{:S(2)}, u32[]{:S(2)}) %collective-permute-start.39) | collective-permute-done | bytes 49184 | tf_op jit(solution)/shard_map/ppermute | solution.py:475
  83.2 2.5 %collective-permute-start.40 = (bf16[64,384]{1,0:T(8,128)(2,1)S(1)}, bf16[64,384]{1,0:T(8,128)(2,1)S(1)}, u32[]{:S(2)}, u32[]{:S(2)}) collective-permute-start(bf16[64,384]{1,0:T(8,128)(2,1)S(1)} %memory_combine.10.a), channel_id=1, source_target_pairs={{0,24},{8,16},{16,8},{24,0},{32,56},{40,48},{48,40},{56,32},{64,88... | collective-permute-start | bytes 147464 | tf_op jit(solution)/shard_map/ppermute | solution.py:479
  87.6 5.1 %collective-permute-start.41 = (bf16[32,512]{1,0:T(8,128)(2,1)S(1)}, bf16[32,512]{1,0:T(8,128)(2,1)S(1)}, u32[]{:S(2)}, u32[]{:S(2)}) collective-permute-start(bf16[32,512]{1,0:T(8,128)(2,1)S(1)} %memory_combine.11), channel_id=1, source_target_pairs={{0,1},{1,0},{2,3},{3,2},{4,5},{5,4},{6,7},{7,6},{8,9},{9,8},{10,11... | collective-permute-start | bytes 98312 | tf_op jit(solution)/shard_map/ppermute | solution.py:503
  92.8 2.5 %collective-permute-start.27 = (bf16[256,512]{1,0:T(8,128)(2,1)S(1)}, bf16[256,512]{1,0:T(8,128)(2,1)S(1)}, u32[]{:S(2)}, u32[]{:S(2)}) collective-permute-start(bf16[256,512]{1,0:T(8,128)(2,1)S(1)} %get-tuple-element.47.kvc), channel_id=1, source_target_pairs={{0,64},{8,72},{16,80},{24,88},{32,96},{40,104},{48,112},{56,120},{... | collective-permute-start | bytes 786440 | tf_op jit(solution)/shard_map/ppermute | solution.py:471
  95.2 3.5 %collective-permute-start.28 = (bf16[256,512]{1,0:T(8,128)(2,1)S(1)}, bf16[256,512]{1,0:T(8,128)(2,1)S(1)}, u32[]{:S(2)}, u32[]{:S(2)}) collective-permute-start(bf16[256,512]{1,0:T(8,128)(2,1)S(1)} %get-tuple-element.47.kvc), channel_id=1, source_target_pairs={{0,32},{8,40},{16,48},{24,56},{32,64},{40,72},{48,80},{56,88},{64,... | collective-permute-start | bytes 786440 | tf_op jit(solution)/shard_map/ppermute | solution.py:471
  100.9 5.6 %collective-permute-done.28.kvb = bf16[256,512]{1,0:T(8,128)(2,1)S(1)} collective-permute-done((bf16[256,512]{1,0:T(8,128)(2,1)S(1)}, bf16[256,512]{1,0:T(8,128)(2,1)S(1)}, u32[]{:S(2)}, u32[]{:S(2)}) %collective-permute-start.28) | collective-permute-done | bytes 262176 | tf_op jit(solution)/shard_map/ppermute | solution.py:471
  106.5 3.6 %token_attention.3 = (bf16[272,512]{1,0:T(8,128)(2,1)S(1)}, bf16[272,512]{1,0:T(8,128)(2,1)S(1)}, bf16[272,512]{1,0:T(8,128)(2,1)S(1)}, bf16[272,512]{1,0:T(8,128)(2,1)S(1)}) custom-call(s32[2,4096]{1,0:T(2,128)S(1)} %copy-done.2, bf16[2,256,512]{2,1,0:T(8,128)(2,1)S(1)} %get-tuple-element.33.q0.q, bf16[2,256,512]{2,1,0:T(8,128)(2,1)S(1)} %collective-permute-done.14.q1, ...), custom_call_target="tpu_custom_call" | custom-call | flops 3000000000 | bytes 4000000 | tf_op jit(solution)/shard_map/token_attention/pallas_call | solution.py:376
  113.2 3.5 %token_attention.2 = (bf16[272,512]{1,0:T(8,128)(2,1)S(1)}, bf16[272,512]{1,0:T(8,128)(2,1)S(1)}, bf16[272,512]{1,0:T(8,128)(2,1)S(1)}, bf16[272,512]{1,0:T(8,128)(2,1)S(1)}) custom-call(s32[2,4096]{1,0:T(2,128)S(1)} %copy-done.2, bf16[2,256,512]{2,1,0:T(8,128)(2,1)S(1)} %get-tuple-element.33.q0.q, bf16[2,256,512]{2,1,0:T(8,128)(2,1)S(1)} %collective-permute-done.14.q1, ...), custom_call_target="tpu_custom_call" | custom-call | flops 3000000000 | bytes 4000000 | tf_op jit(solution)/shard_map/token_attention/pallas_call | solution.py:376
  116.8 2.5 %collective-permute-start.17 = (bf16[272,512]{1,0:T(8,128)(2,1)S(1)}, bf16[272,512]{1,0:T(8,128)(2,1)S(1)}, u32[]{:S(2)}, u32[]{:S(2)}) collective-permute-start(bf16[272,512]{1,0:T(8,128)(2,1)S(1)} %get-tuple-element.42), channel_id=1, source_target_pairs={{0,24},{8,0},{16,8},{24,16},{32,56},{40,32},{48,40},{56,48},{64,88... | collective-permute-start | bytes 835592 | tf_op jit(solution)/shard_map/ppermute | solution.py:461
  122.5 3.0 %collective-permute-start.44 = (bf16[32,1792]{1,0:T(8,128)(2,1)S(1)}, bf16[32,1792]{1,0:T(8,128)(2,1)S(1)}, u32[]{:S(2)}, u32[]{:S(2)}) collective-permute-start(bf16[32,1792]{1,0:T(8,128)(2,1)S(1)} %get-tuple-element.55), channel_id=1, source_target_pairs={{0,1},{1,0},{2,3},{3,2},{4,5},{5,4},{6,7},{7,6},{8,9},{9,8},{10,11... | collective-permute-start | bytes 344072 | tf_op jit(solution)/shard_map/ppermute | solution.py:503
  132.7 3.7 %collective-permute-start.32 = (bf16[256,512]{1,0:T(8,128)(2,1)S(1)}, bf16[256,512]{1,0:T(8,128)(2,1)S(1)}, u32[]{:S(2)}, u32[]{:S(2)}) collective-permute-start(bf16[256,512]{1,0:T(8,128)(2,1)S(1)} %token_combine.3.refs_0_), channel_id=1, source_target_pairs={{0,1},{1,0},{2,3},{3,2},{4,5},{5,4},{6,7},{7,6},{8,9},{9,8},{10,11... | collective-permute-start | bytes 786440 | tf_op jit(solution)/shard_map/ppermute | solution.py:503
  136.4 2.4 %collective-permute-done.19.d = bf16[272,512]{1,0:T(8,128)(2,1)S(1)} collective-permute-done((bf16[272,512]{1,0:T(8,128)(2,1)S(1)}, bf16[272,512]{1,0:T(8,128)(2,1)S(1)}, u32[]{:S(2)}, u32[]{:S(2)}) %collective-permute-start.19) | collective-permute-done | bytes 278560 | tf_op jit(solution)/shard_map/ppermute | solution.py:461
  144.4 3.2 %collective-permute-start.25 = (bf16[256,512]{1,0:T(8,128)(2,1)S(1)}, bf16[256,512]{1,0:T(8,128)(2,1)S(1)}, u32[]{:S(2)}, u32[]{:S(2)}) collective-permute-start(bf16[256,512]{1,0:T(8,128)(2,1)S(1)} %token_combine.2.refs_0_), channel_id=1, source_target_pairs={{0,6},{1,7},{2,0},{3,1},{4,2},{5,3},{6,4},{7,5},{8,14},{9,15},{10,... | collective-permute-start | bytes 786440 | tf_op jit(solution)/shard_map/ppermute | solution.py:499
  151.9 5.4 %collective-permute-done.23.refs_4_ = bf16[256,512]{1,0:T(8,128)(2,1)S(1)} collective-permute-done((bf16[256,512]{1,0:T(8,128)(2,1)S(1)}, bf16[256,512]{1,0:T(8,128)(2,1)S(1)}, u32[]{:S(2)}, u32[]{:S(2)}) %collective-permute-start.23) | collective-permute-done | bytes 262176 | tf_op jit(solution)/shard_map/ppermute | solution.py:499
  (108 shorter events, 66.4 us)
Async XLA Ops:
  51.1 14.4 %collective-permute-start.12 = (bf16[256,512]{1,0:T(8,128)(2,1)S(1)}, bf16[256,512]{1,0:T(8,128)(2,1)S(1)}, u32[]{:S(2)}, u32[]{:S(2)}) collective-permute-start(bf16[256,512]{1,0:T(8,128)(2,1)S(1)} %get-tuple-element.39.refs_0_.kvc), channel_id=1, source_target_pairs={{0,64},{8,72},{16,80},{24,88},{32,96},{40,104},{48,112},{56,120},{... | collective-permute-start | bytes 786440 | tf_op jit(solution)/shard_map/ppermute | solution.py:467
  54.9 13.0 %collective-permute-start.13 = (bf16[256,512]{1,0:T(8,128)(2,1)S(1)}, bf16[256,512]{1,0:T(8,128)(2,1)S(1)}, u32[]{:S(2)}, u32[]{:S(2)}) collective-permute-start(bf16[256,512]{1,0:T(8,128)(2,1)S(1)} %get-tuple-element.39.refs_0_.kvc), channel_id=1, source_target_pairs={{0,96},{8,104},{16,112},{24,120},{32,0},{40,8},{48,16},{56,24},{64... | collective-permute-start | bytes 786440 | tf_op jit(solution)/shard_map/ppermute | solution.py:467
  55.0 13.0 %collective-permute-start.10 = (bf16[32,1792]{1,0:T(8,128)(2,1)S(1)}, bf16[32,1792]{1,0:T(8,128)(2,1)S(1)}, u32[]{:S(2)}, u32[]{:S(2)}) collective-permute-start(bf16[32,1792]{1,0:T(8,128)(2,1)S(1)} %add_convert_fusion.3.own), channel_id=1, source_target_pairs={{0,1},{1,0},{2,3},{3,2},{4,5},{5,4},{6,7},{7,6},{8,9},{9,8},{10,11... | collective-permute-start | bytes 344072 | tf_op jit(solution)/shard_map/ppermute | solution.py:503
  57.3 49.2 %collective-permute-start.14 = (bf16[2,256,512]{2,1,0:T(8,128)(2,1)S(1)}, bf16[2,256,512]{2,1,0:T(8,128)(2,1)S(1)}, u32[]{:S(2)}, u32[]{:S(2)}) collective-permute-start(bf16[2,256,512]{2,1,0:T(8,128)(2,1)S(1)} %get-tuple-element.33.q0.q), channel_id=1, source_target_pairs={{0,8},{8,16},{16,24},{24,0},{32,40},{40,48},{48,56},{56,32},{64,72... | collective-permute-start | bytes 1572872 | tf_op jit(solution)/shard_map/ppermute | solution.py:461
  58.7 47.8 %collective-permute-start.15 = (bf16[2,256,512]{2,1,0:T(8,128)(2,1)S(1)}, bf16[2,256,512]{2,1,0:T(8,128)(2,1)S(1)}, u32[]{:S(2)}, u32[]{:S(2)}) collective-permute-start(bf16[2,256,512]{2,1,0:T(8,128)(2,1)S(1)} %get-tuple-element.33.q0.q), channel_id=1, source_target_pairs={{0,16},{8,24},{16,0},{24,8},{32,48},{40,56},{48,32},{56,40},{64,80... | collective-permute-start | bytes 1572872 | tf_op jit(solution)/shard_map/ppermute | solution.py:461
  65.4 41.1 %collective-permute-start.16 = (bf16[2,256,512]{2,1,0:T(8,128)(2,1)S(1)}, bf16[2,256,512]{2,1,0:T(8,128)(2,1)S(1)}, u32[]{:S(2)}, u32[]{:S(2)}) collective-permute-start(bf16[2,256,512]{2,1,0:T(8,128)(2,1)S(1)} %get-tuple-element.33.q0.q), channel_id=1, source_target_pairs={{0,24},{8,0},{16,8},{24,16},{32,56},{40,32},{48,40},{56,48},{64,88... | collective-permute-start | bytes 1572872 | tf_op jit(solution)/shard_map/ppermute | solution.py:461
  70.3 12.7 %collective-permute-start.39 = (bf16[64,384]{1,0:T(8,128)(2,1)S(1)}, bf16[64,384]{1,0:T(8,128)(2,1)S(1)}, u32[]{:S(2)}, u32[]{:S(2)}) collective-permute-start(bf16[64,384]{1,0:T(8,128)(2,1)S(1)} %get-tuple-element.52.a), channel_id=1, source_target_pairs={{0,8},{8,0},{16,24},{24,16},{32,40},{40,32},{48,56},{56,48},{64,72... | collective-permute-start | bytes 147464 | tf_op jit(solution)/shard_map/ppermute | solution.py:475
  95.2 11.3 %collective-permute-start.28 = (bf16[256,512]{1,0:T(8,128)(2,1)S(1)}, bf16[256,512]{1,0:T(8,128)(2,1)S(1)}, u32[]{:S(2)}, u32[]{:S(2)}) collective-permute-start(bf16[256,512]{1,0:T(8,128)(2,1)S(1)} %get-tuple-element.47.kvc), channel_id=1, source_target_pairs={{0,32},{8,40},{16,48},{24,56},{32,64},{40,72},{48,80},{56,88},{64,... | collective-permute-start | bytes 786440 | tf_op jit(solution)/shard_map/ppermute | solution.py:471
  100.9 10.7 %collective-permute-start.42 = (bf16[2,32,512]{2,1,0:T(8,128)(2,1)S(1)}, bf16[2,32,512]{2,1,0:T(8,128)(2,1)S(1)}, u32[]{:S(2)}, u32[]{:S(2)}) collective-permute-start(bf16[2,32,512]{2,1,0:T(8,128)(2,1)S(1)} %pad_maximum_fusion.5), channel_id=1, source_target_pairs={{0,2},{1,3},{2,0},{3,1},{4,6},{5,7},{6,4},{7,5},{8,10},{9,11},{10,... | collective-permute-start | bytes 196616 | tf_op jit(solution)/shard_map/ppermute | solution.py:491
  110.1 12.4 %collective-permute-start.29 = (bf16[272,512]{1,0:T(8,128)(2,1)S(1)}, bf16[272,512]{1,0:T(8,128)(2,1)S(1)}, u32[]{:S(2)}, u32[]{:S(2)}) collective-permute-start(bf16[272,512]{1,0:T(8,128)(2,1)S(1)} %get-tuple-element.49), channel_id=1, source_target_pairs={{0,24},{8,0},{16,8},{24,16},{32,56},{40,32},{48,40},{56,48},{64,88... | collective-permute-start | bytes 835592 | tf_op jit(solution)/shard_map/ppermute | solution.py:461
  110.8 14.7 %collective-permute-start.30 = (bf16[272,512]{1,0:T(8,128)(2,1)S(1)}, bf16[272,512]{1,0:T(8,128)(2,1)S(1)}, u32[]{:S(2)}, u32[]{:S(2)}) collective-permute-start(bf16[272,512]{1,0:T(8,128)(2,1)S(1)} %get-tuple-element.50), channel_id=1, source_target_pairs={{0,16},{8,24},{16,0},{24,8},{32,48},{40,56},{48,32},{56,40},{64,80... | collective-permute-start | bytes 835592 | tf_op jit(solution)/shard_map/ppermute | solution.py:461
  110.8 17.5 %collective-permute-start.31 = (bf16[272,512]{1,0:T(8,128)(2,1)S(1)}, bf16[272,512]{1,0:T(8,128)(2,1)S(1)}, u32[]{:S(2)}, u32[]{:S(2)}) collective-permute-start(bf16[272,512]{1,0:T(8,128)(2,1)S(1)} %get-tuple-element.51), channel_id=1, source_target_pairs={{0,8},{8,16},{16,24},{24,0},{32,40},{40,48},{48,56},{56,32},{64,72... | collective-permute-start | bytes 835592 | tf_op jit(solution)/shard_map/ppermute | solution.py:461
  116.8 13.6 %collective-permute-start.17 = (bf16[272,512]{1,0:T(8,128)(2,1)S(1)}, bf16[272,512]{1,0:T(8,128)(2,1)S(1)}, u32[]{:S(2)}, u32[]{:S(2)}) collective-permute-start(bf16[272,512]{1,0:T(8,128)(2,1)S(1)} %get-tuple-element.42), channel_id=1, source_target_pairs={{0,24},{8,0},{16,8},{24,16},{32,56},{40,32},{48,40},{56,48},{64,88... | collective-permute-start | bytes 835592 | tf_op jit(solution)/shard_map/ppermute | solution.py:461
  119.3 12.8 %collective-permute-start.18 = (bf16[272,512]{1,0:T(8,128)(2,1)S(1)}, bf16[272,512]{1,0:T(8,128)(2,1)S(1)}, u32[]{:S(2)}, u32[]{:S(2)}) collective-permute-start(bf16[272,512]{1,0:T(8,128)(2,1)S(1)} %get-tuple-element.43), channel_id=1, source_target_pairs={{0,16},{8,24},{16,0},{24,8},{32,48},{40,56},{48,32},{56,40},{64,80... | collective-permute-start | bytes 835592 | tf_op jit(solution)/shard_map/ppermute | solution.py:461
  125.5 13.3 %collective-permute-start.19 = (bf16[272,512]{1,0:T(8,128)(2,1)S(1)}, bf16[272,512]{1,0:T(8,128)(2,1)S(1)}, u32[]{:S(2)}, u32[]{:S(2)}) collective-permute-start(bf16[272,512]{1,0:T(8,128)(2,1)S(1)} %get-tuple-element.44), channel_id=1, source_target_pairs={{0,8},{8,16},{16,24},{24,0},{32,40},{40,48},{48,56},{56,32},{64,72... | collective-permute-start | bytes 835592 | tf_op jit(solution)/shard_map/ppermute | solution.py:461
  129.6 10.5 %collective-permute-start.33 = (bf16[256,512]{1,0:T(8,128)(2,1)S(1)}, bf16[256,512]{1,0:T(8,128)(2,1)S(1)}, u32[]{:S(2)}, u32[]{:S(2)}) collective-permute-start(bf16[256,512]{1,0:T(8,128)(2,1)S(1)} %token_combine.3.refs_0_), channel_id=1, source_target_pairs={{0,2},{1,3},{2,4},{3,5},{4,6},{5,7},{6,0},{7,1},{8,10},{9,11},{10,... | collective-permute-start | bytes 786440 | tf_op jit(solution)/shard_map/ppermute | solution.py:499
  130.4 13.1 %collective-permute-start.35 = (bf16[256,512]{1,0:T(8,128)(2,1)S(1)}, bf16[256,512]{1,0:T(8,128)(2,1)S(1)}, u32[]{:S(2)}, u32[]{:S(2)}) collective-permute-start(bf16[256,512]{1,0:T(8,128)(2,1)S(1)} %token_combine.3.refs_0_), channel_id=1, source_target_pairs={{0,4},{1,5},{2,6},{3,7},{4,0},{5,1},{6,2},{7,3},{8,12},{9,13},{10,... | collective-permute-start | bytes 786440 | tf_op jit(solution)/shard_map/ppermute | solution.py:499
  132.0 12.4 %collective-permute-start.37 = (bf16[256,512]{1,0:T(8,128)(2,1)S(1)}, bf16[256,512]{1,0:T(8,128)(2,1)S(1)}, u32[]{:S(2)}, u32[]{:S(2)}) collective-permute-start(bf16[256,512]{1,0:T(8,128)(2,1)S(1)} %token_combine.3.refs_0_), channel_id=1, source_target_pairs={{0,6},{1,7},{2,0},{3,1},{4,2},{5,3},{6,4},{7,5},{8,14},{9,15},{10,... | collective-permute-start | bytes 786440 | tf_op jit(solution)/shard_map/ppermute | solution.py:499
  132.7 14.9 %collective-permute-start.32 = (bf16[256,512]{1,0:T(8,128)(2,1)S(1)}, bf16[256,512]{1,0:T(8,128)(2,1)S(1)}, u32[]{:S(2)}, u32[]{:S(2)}) collective-permute-start(bf16[256,512]{1,0:T(8,128)(2,1)S(1)} %token_combine.3.refs_0_), channel_id=1, source_target_pairs={{0,1},{1,0},{2,3},{3,2},{4,5},{5,4},{6,7},{7,6},{8,9},{9,8},{10,11... | collective-permute-start | bytes 786440 | tf_op jit(solution)/shard_map/ppermute | solution.py:503
  140.2 10.3 %collective-permute-start.21 = (bf16[256,512]{1,0:T(8,128)(2,1)S(1)}, bf16[256,512]{1,0:T(8,128)(2,1)S(1)}, u32[]{:S(2)}, u32[]{:S(2)}) collective-permute-start(bf16[256,512]{1,0:T(8,128)(2,1)S(1)} %token_combine.2.refs_0_), channel_id=1, source_target_pairs={{0,2},{1,3},{2,4},{3,5},{4,6},{5,7},{6,0},{7,1},{8,10},{9,11},{10,... | collective-permute-start | bytes 786440 | tf_op jit(solution)/shard_map/ppermute | solution.py:499
  143.5 13.7 %collective-permute-start.23 = (bf16[256,512]{1,0:T(8,128)(2,1)S(1)}, bf16[256,512]{1,0:T(8,128)(2,1)S(1)}, u32[]{:S(2)}, u32[]{:S(2)}) collective-permute-start(bf16[256,512]{1,0:T(8,128)(2,1)S(1)} %token_combine.2.refs_0_), channel_id=1, source_target_pairs={{0,4},{1,5},{2,6},{3,7},{4,0},{5,1},{6,2},{7,3},{8,12},{9,13},{10,... | collective-permute-start | bytes 786440 | tf_op jit(solution)/shard_map/ppermute | solution.py:499
  144.4 14.3 %collective-permute-start.25 = (bf16[256,512]{1,0:T(8,128)(2,1)S(1)}, bf16[256,512]{1,0:T(8,128)(2,1)S(1)}, u32[]{:S(2)}, u32[]{:S(2)}) collective-permute-start(bf16[256,512]{1,0:T(8,128)(2,1)S(1)} %token_combine.2.refs_0_), channel_id=1, source_target_pairs={{0,6},{1,7},{2,0},{3,1},{4,2},{5,3},{6,4},{7,5},{8,14},{9,15},{10,... | collective-permute-start | bytes 786440 | tf_op jit(solution)/shard_map/ppermute | solution.py:499
  147.6 12.0 %collective-permute-start.34 = (bf16[256,512]{1,0:T(8,128)(2,1)S(1)}, bf16[256,512]{1,0:T(8,128)(2,1)S(1)}, u32[]{:S(2)}, u32[]{:S(2)}) collective-permute-start(bf16[256,512]{1,0:T(8,128)(2,1)S(1)} %collective-permute-done.33.refs_2_), channel_id=1, source_target_pairs={{0,1},{1,0},{2,3},{3,2},{4,5},{5,4},{6,7},{7,6},{8,9},{9,8},{10,11... | collective-permute-start | bytes 786440 | tf_op jit(solution)/shard_map/ppermute | solution.py:503
  148.5 11.1 %collective-permute-start.36 = (bf16[256,512]{1,0:T(8,128)(2,1)S(1)}, bf16[256,512]{1,0:T(8,128)(2,1)S(1)}, u32[]{:S(2)}, u32[]{:S(2)}) collective-permute-start(bf16[256,512]{1,0:T(8,128)(2,1)S(1)} %collective-permute-done.35.refs_4_), channel_id=1, source_target_pairs={{0,1},{1,0},{2,3},{3,2},{4,5},{5,4},{6,7},{7,6},{8,9},{9,8},{10,11... | collective-permute-start | bytes 786440 | tf_op jit(solution)/shard_map/ppermute | solution.py:503
  (27 other events, 187.2 us)
where the time goes:
time: 167 us; the launch traced here: 166 us
  starting transfers between devices  77.3 us (46%)
  waiting for transfers between devices  55 us (33%)
  Pallas kernels  31.4 us (19%)
    ppermute x14, starting transfers between devices, other_core(): return lax.ppermute(v, 'head', [(i, i ^ 1) for i in range(N_HEAD)])  27.6 us
    ppermute x2, waiting for transfers between devices, x_near(): return lax.ppermute(v, 'seq', [(i, i ^ 1) for i in range(N_SEQ)])  14 us
    ppermute x9, starting transfers between devices, x_shift(): lax.ppermute(v, 'seq', [(i, i // SHAPE * SHAPE + (i + d) % SHAPE) for i i...  10.4 us
    ppermute x6, starting transfers between devices, z_shift(): lax.ppermute(v, 'head', [(i, (i + 2 * d) % N_HEAD) for i in range(N_HEAD)])  8.04 us
    ppermute x2, waiting for transfers between devices, y_later(): lax.ppermute(v, 'seq', [(i, i + d * SHAPE) for i in range(N_SEQ - d * SHA...  7.7 us
    ppermute x4, starting transfers between devices, z_far(): return lax.ppermute(v, 'head', [(i, i ^ 6) for i in range(N_HEAD)])  7.31 us
    ppermute x6, waiting for transfers between devices, z_shift(): lax.ppermute(v, 'head', [(i, (i + 2 * d) % N_HEAD) for i in range(N_HEAD)])  7.2 us
    pallas_call x2, Pallas kernels, token_attention(): pl.pallas_call(functools.partial(token_kernel, seg), in_specs=[WHOLE] * 8...  7.1 us
  transfers between devices with their start and end apart: 48, of which 20 were waited for; matrix products, arithmetic and copies ran while one was open for 0% of the time, Pallas kernels for 14%

commit v1 on v0

--- a/solution.py
+++ b/solution.py
@@ -168,7 +168,7 @@
     return pl.multiple_of((h * 7 // 2) * 128, 128)
 
 
-def second_kernel(x, gain, wq, wk, wv, q0, wt, proj, *refs):
+def second_kernel(x, gain, wq, wk, wv, wt, proj, *refs):
     q_ref, kv_ref, wt_buf, proj_buf, cols_buf, xs, squares, acc, sems, wsems = refs
     _, _, z, c = place()
     copies = []
@@ -187,7 +187,6 @@
     ]
     for c in copies + late:
         c.start()
-    q_ref[0] = q0[...]
     g = gain[...].astype(F32).reshape(1, D)
     for k, c in enumerate(copies):
         c.wait()
@@ -195,18 +194,18 @@
         a = scaled_chunk(xs[:, span], g[:, span], squares, slice(0, ROWS), k == 0)
         accumulate(acc, a, [w[span, :] for w in (wq, wk, wv)], k == 0)
     out = (acc[...] * norm_of(squares)).astype(BF)
-    q_ref[1] = out[:, : 2 * HD]
+    q_ref[...] = out[:, : 2 * HD]
     kv_ref[...] = out[:, 2 * HD :]
     for c in late:
         c.wait()
 
 
-def second_project(x, gain, wq, wk, wv, q0, wt, proj):
+def second_project(x, gain, wq, wk, wv, wt, proj):
     hbm = pl.BlockSpec(memory_space=pltpu.HBM)
-    shapes = [(2, ROWS, 2 * HD), (ROWS, 2 * HD), wt.shape, proj.shape, (2, ROWS, 512)]
+    shapes = [(ROWS, 2 * HD), (ROWS, 2 * HD), wt.shape, proj.shape, (2, ROWS, 512)]
     return pl.pallas_call(
         second_kernel,
-        in_specs=[hbm] + [WHOLE] * 5 + [hbm, hbm],
+        in_specs=[hbm] + [WHOLE] * 4 + [hbm, hbm],
         out_specs=[WHOLE] * len(shapes),
         out_shape=[jax.ShapeDtypeStruct(s, BF) for s in shapes],
         scratch_shapes=[
@@ -221,7 +220,7 @@
             flops=2 * ROWS * D * 4 * HD, bytes_accessed=10 * 2**20, transcendentals=512
         ),
         name="second_project",
-    )(x, gain, wq, wk, wv, q0, wt, proj)
+    )(x, gain, wq, wk, wv, wt, proj)
 
 
 def memory_project_kernel(own, other, gain, wq, wk, wv, *refs):
@@ -286,16 +285,44 @@
     )(a, b)
 
 
-def memory_write_kernel(blocks, mem, w_out, proj, keep_ref, send_ref):
+def pair_kernel(a, b, out_ref):
+    out_ref[0] = a[...]
+    out_ref[1] = b[...]
+
+
+def pair_up(a, b):
+    return pl.pallas_call(
+        pair_kernel,
+        in_specs=[WHOLE] * 2,
+        out_specs=WHOLE,
+        out_shape=jax.ShapeDtypeStruct((2, *a.shape), BF),
+        compiler_params=params(4),
+        name="pair_up",
+    )(a, b)
+
+
+def gathered_heads():
+    _, _, z, c = place()
+    side = 1 - 2 * c
+    before, after = lax.rem(z - side + SHAPE, SHAPE), lax.rem(z + side + SHAPE, SHAPE)
+    far = lax.rem(z + 2, SHAPE)
+    chips = (z, z, before, before, after, after, far, far)
+    cores = (c, 1 - c, c, 1 - c, 1 - c, c, c, 1 - c)
+    return [2 * zz + cc for zz, cc in zip(chips, cores)]
+
+
+def block_values(refs):
+    own, swapped, near, near2, far = refs[:5]
+    last = [far[0], far[1]] if len(refs) == 5 else [far[...], refs[5][...]]
+    return [own[...], swapped[...], near[0], near[1], near2[0], near2[1], *last]
+
+
+def memory_write_kernel(o, o2, n, n2, f, f2, mem, w_out, proj, keep_ref, send_ref):
     _, _, z, c = place()
     wide = mem[:, pl.ds(window(2 * z + c), 512)].astype(F32)
     acc = jnp.where(c == 1, wide[:, 64:], wide[:, :COLS])
-    far = SHAPE - 1 - z
-    for k, zz in enumerate((z, flip(z), far, flip(far))):
-        for e in range(2):
-            h = zz * 2 + (c if e == 0 else 1 - c)
-            w = w_out[:, pl.ds(pl.multiple_of(h * 2 * HD, 2 * HD), 2 * HD)]
-            acc = acc + dot_t(blocks[2 * k + e], w)
+    for h, v in zip(gathered_heads(), block_values((o, o2, n, n2, f, f2))):
+        acc = acc + dot_t(v, w_out[:, pl.ds(pl.multiple_of(h * 2 * HD, 2 * HD), 2 * HD)])
     a = acc.astype(BF)
     keep_ref[...] = dot(a, proj[:, pl.ds(pl.multiple_of(c * HALF, 128), HALF)]).astype(BF)
     send_ref[...] = dot(a, proj[:, pl.ds(pl.multiple_of((1 - c) * HALF, 128), HALF)]).astype(BF)
@@ -318,14 +345,10 @@
     )(own, other)
 
 
-def flip(i):
-    return i + 1 - 2 * lax.rem(i, 2)
-
-
 def memory_write(blocks, mem, w_out, proj):
     return pl.pallas_call(
         memory_write_kernel,
-        in_specs=[WHOLE] * 4,
+        in_specs=[WHOLE] * 9,
         out_specs=[WHOLE] * 2,
         out_shape=[jax.ShapeDtypeStruct((M, HALF), BF)] * 2,
         compiler_params=params(20),
@@ -333,21 +356,24 @@
             flops=2 * 256 * D * 8 * COLS, bytes_accessed=8 * 1024 * 1024, transcendentals=0
         ),
         name="memory_write",
-    )(blocks, mem, w_out, proj)
-
-
-def token_kernel(seg, docs, q0, q1, q2, q3, kva, kvb, kvc, o0, o1, o2, o3, kvs, kcode):
+    )(*blocks, mem, w_out, proj)
+
+
+def token_kernel(seg, docs, q0, q1, q2, q3, kva, kvb, kvb2, kvc, o0, o1, o2, o3, kvs, kcode):
     x, y, _, _ = place()
     lane = lax.broadcasted_iota(jnp.int32, (1, ROWS), 1).astype(F32)
     for n, ref in enumerate((kva, kvb, kvc)):
-        kvs[n * ROWS : (n + 1) * ROWS, :] = ref[...]
+        if n == 1:
+            kvs[ROWS : 2 * ROWS, :] = jnp.where(y % 2 == 1, kvb[...], kvb2[...])
+        else:
+            kvs[n * ROWS : (n + 1) * ROWS, :] = ref[...]
         block = (y - 2 + n) * SHAPE + x
         start = jnp.maximum(block, 0) * ROWS
         doc = docs[seg : seg + 1, pl.ds(pl.multiple_of(start, ROWS), ROWS)].astype(F32)
         code = doc * 4096.0 + lane + start.astype(F32)
         kcode[:, n * ROWS : (n + 1) * ROWS] = jnp.where(block >= 0, code, -1.0)
     for d, (q_ref, o_ref) in enumerate(zip((q0, q1, q2, q3), (o0, o1, o2, o3))):
-        start = (y * SHAPE + lax.rem(x - d + SHAPE, SHAPE)) * ROWS
+        start = (y * SHAPE + lax.bitwise_xor(x, d)) * ROWS
         doc = docs[seg : seg + 1, pl.ds(pl.multiple_of(start, ROWS), ROWS)].astype(F32)
         low = column(doc * 4096.0)
         high = column(doc * 4096.0 + lane + start.astype(F32))
@@ -355,13 +381,13 @@
             codes = kcode[...]
             keys = kvs[...]
         else:
-            at = jnp.where(x >= d, 0, ROWS)
+            at = jnp.where(lax.bitwise_xor(x, d) < x, 0, ROWS)
             at = pl.multiple_of(at, ROWS)
             codes = kcode[:, pl.ds(at, 2 * ROWS)]
             keys = kvs[pl.ds(at, 2 * ROWS), :]
         valid = (codes >= low) & (codes <= high)
         for g in range(2):
-            q = q_ref[seg, :, g * HD : (g + 1) * HD]
+            q = q_ref[:, g * HD : (g + 1) * HD]
             scores = jnp.where(valid, dot_t(q, keys[:, :HD]) * LOG2E_SCALE, LOW)
             out, lse = attend([scores], [keys[:, HD:]])
             row = as_row(lse)
@@ -372,10 +398,10 @@
             o_ref[ROWS:, g * HD : (g + 1) * HD] = stats.astype(BF)
 
 
-def token_attention(docs, seg, qs, kva, kvb, kvc):
+def token_attention(docs, seg, qs, kva, kvb, kvb2, kvc):
     return pl.pallas_call(
         functools.partial(token_kernel, seg),
-        in_specs=[WHOLE] * 8,
+        in_specs=[WHOLE] * 9,
         out_specs=[WHOLE] * 4,
         out_shape=[jax.ShapeDtypeStruct((ROWS + 16, 2 * HD), BF)] * 4,
         scratch_shapes=[pltpu.VMEM((3 * ROWS, 2 * HD), BF), pltpu.VMEM((1, 3 * ROWS), F32)],
@@ -384,14 +410,14 @@
             flops=3 * 10**9, bytes_accessed=4 * 10**6, transcendentals=10**6
         ),
         name="token_attention",
-    )(docs, *qs, kva, kvb, kvc)
-
-
-def token_combine_kernel(seg, q, qkvm, a, b, c, d, out_ref):
+    )(docs, *qs, kva, kvb, kvb2, kvc)
+
+
+def token_combine_kernel(q, qkvm, a, b, c, d, out_ref):
     refs = (a, b, c, d)
     for g in range(2):
         lanes = slice(g * HD, (g + 1) * HD)
-        scores = dot_t(q[seg, :, lanes], qkvm[:, 2 * HD : 3 * HD]) * LOG2E_SCALE
+        scores = dot_t(q[:, lanes], qkvm[:, 2 * HD : 3 * HD]) * LOG2E_SCALE
         out, lse = attend([scores], [qkvm[:, 3 * HD :]])
         outs, lses = [out], [lse]
         for r in refs:
@@ -404,9 +430,9 @@
         out_ref[:, lanes] = mixed.astype(BF)
 
 
-def token_combine(seg, q, qkvm, parts):
-    return pl.pallas_call(
-        functools.partial(token_combine_kernel, seg),
+def token_combine(q, qkvm, parts):
+    return pl.pallas_call(
+        token_combine_kernel,
         in_specs=[WHOLE] * 6,
         out_specs=WHOLE,
         out_shape=jax.ShapeDtypeStruct((ROWS, 2 * HD), BF),
@@ -417,58 +443,102 @@
 
 
 def token_out_kernel(seg, *refs):
-    blocks, cols, w_out, out_ref, flat = refs[:8], refs[8], refs[9], refs[-2], refs[-1]
-    _, _, z, c = place()
-    acc = jnp.zeros((COLS, ROWS), F32)
-    for n, ref in enumerate(blocks):
-        k, e = n // 2, n % 2
-        h = lax.rem(z - k + SHAPE, SHAPE) * 2 + (c if e == 0 else 1 - c)
-        w = w_out[:, pl.ds(pl.multiple_of(h * 2 * HD, 2 * HD), 2 * HD)]
-        acc = acc + dot_t(w, ref[...])
+    blocks, cols, w_out, out_ref, flat = refs[:5], *refs[5:]
+    acc = features(cols, seg, flat)
+    for h, v in zip(gathered_heads(), block_values(blocks)):
+        acc = acc + dot_t(w_out[:, pl.ds(pl.multiple_of(h * 2 * HD, 2 * HD), 2 * HD)], v)
+    out_ref[0] = acc.astype(BF)
+
+
+def features(cols, seg, flat):
+    _, _, _, c = place()
     for at in range(0, 512, 128):
         flat[at : at + 128, :] = cols[seg, :, at : at + 128].astype(F32).T
-    out_ref[0] = (acc + flat[pl.ds(pl.multiple_of(c * 64, 64), COLS), :]).astype(BF)
-
-
-def token_out(blocks, cols, seg, w_out, before):
-    in_specs = [WHOLE] * 10
-    args = [*blocks, cols, w_out]
-    aliases = {}
-    if before is not None:
-        in_specs.append(pl.BlockSpec(memory_space=pl.ANY))
-        args.append(before)
-        aliases = {len(args) - 1: 0}
+    return flat[pl.ds(pl.multiple_of(c * 64, 64), COLS), :]
+
+
+def token_out(blocks, cols, seg, w_out):
     return pl.pallas_call(
         functools.partial(token_out_kernel, seg),
         grid=(1,),
-        in_specs=in_specs,
+        in_specs=[WHOLE] * 7,
         out_specs=pl.BlockSpec((1, COLS, ROWS), lambda k: (seg, 0, 0)),
         out_shape=jax.ShapeDtypeStruct((2, COLS, ROWS), BF),
-        input_output_aliases=aliases,
         scratch_shapes=[pltpu.VMEM((512, ROWS), F32)],
         compiler_params=params(12),
         cost_estimate=pl.CostEstimate(
             flops=2 * ROWS * 4096 * COLS, bytes_accessed=6 * 10**6, transcendentals=0
         ),
         name="token_out",
-    )(*args)
+    )(*blocks, cols, w_out)
+
+
+def early_kernel(seg, *refs):
+    cols, w_out, out_ref, flat = refs[4:]
+    own, swapped, near, near2 = refs[:4]
+    values = [own[...], swapped[...], near[0], near[1], near2[0], near2[1]]
+    acc = features(cols, seg, flat)
+    for h, v in zip(gathered_heads(), values):
+        acc = acc + dot_t(w_out[:, pl.ds(pl.multiple_of(h * 2 * HD, 2 * HD), 2 * HD)], v)
+    out_ref[...] = acc
+
+
+def token_out_early(blocks, cols, seg, w_out):
+    return pl.pallas_call(
+        functools.partial(early_kernel, seg),
+        in_specs=[WHOLE] * 6,
+        out_specs=WHOLE,
+        out_shape=jax.ShapeDtypeStruct((COLS, ROWS), F32),
+        scratch_shapes=[pltpu.VMEM((512, ROWS), F32)],
+        compiler_params=params(12),
+        cost_estimate=pl.CostEstimate(
+            flops=2 * ROWS * 3072 * COLS, bytes_accessed=5 * 10**6, transcendentals=0
+        ),
+        name="token_out_early",
+    )(*blocks, cols, w_out)
+
+
+def late_kernel(far, early, w_out, before, out_ref):
+    acc = early[...]
+    for h, v in zip(gathered_heads()[6:], (far[0], far[1])):
+        acc = acc + dot_t(w_out[:, pl.ds(pl.multiple_of(h * 2 * HD, 2 * HD), 2 * HD)], v)
+    out_ref[0] = acc.astype(BF)
+
+
+def token_out_late(far, early, seg, w_out, before):
+    return pl.pallas_call(
+        late_kernel,
+        grid=(1,),
+        in_specs=[WHOLE] * 3 + [pl.BlockSpec(memory_space=pl.ANY)],
+        out_specs=pl.BlockSpec((1, COLS, ROWS), lambda k: (seg, 0, 0)),
+        out_shape=jax.ShapeDtypeStruct((2, COLS, ROWS), BF),
+        input_output_aliases={3: 0},
+        compiler_params=params(12),
+        cost_estimate=pl.CostEstimate(
+            flops=2 * ROWS * 1024 * COLS, bytes_accessed=3 * 10**6, transcendentals=0
+        ),
+        name="token_out_late",
+    )(far, early, w_out, before)
 
 
 N_SEQ, N_HEAD = SHAPE * SHAPE, 8
 
 
-def x_shift(v, d):
-    return lax.ppermute(
-        v, "seq", [(i, i // SHAPE * SHAPE + (i + d) % SHAPE) for i in range(N_SEQ)]
-    )
-
-
-def y_shift(v, d):
-    return lax.ppermute(v, "seq", [(i, (i + d * SHAPE) % N_SEQ) for i in range(N_SEQ)])
-
-
-def y_later(v, d):
-    return lax.ppermute(v, "seq", [(i, i + d * SHAPE) for i in range(N_SEQ - d * SHAPE)])
+def x_xor(v, d):
+    return lax.ppermute(v, "seq", [(i, i ^ d) for i in range(N_SEQ)])
+
+
+def y_xor(v, d):
+    return x_xor(v, 4 * d)
+
+
+def y_later(v):
+    return lax.ppermute(v, "seq", [(i, i + SHAPE) for i in range(N_SEQ - SHAPE)])
+
+
+def all_four(send, v):
+    near = send(v, 1)
+    return [v, near, send(near, 3), send(v, 3)]
 
 
 def x_near(v):
@@ -495,8 +565,12 @@
     return lax.ppermute(v, "head", [(i, i ^ 6) for i in range(N_HEAD)])
 
 
-def z_shift(v, d):
-    return lax.ppermute(v, "head", [(i, (i + 2 * d) % N_HEAD) for i in range(N_HEAD)])
+def z_turn(v):
+    return lax.ppermute(v, "head", [(i, (i + 2 - 4 * (i % 2)) % N_HEAD) for i in range(N_HEAD)])
+
+
+def z_two(v):
+    return lax.ppermute(v, "head", [(i, (i + 4) % N_HEAD) for i in range(N_HEAD)])
 
 
 def other_core(v):
@@ -507,10 +581,23 @@
     return (a.astype(F32) + b.astype(F32)).astype(BF)
 
 
+def gather_heads(v):
+    far = z_two(v)
+    swapped = other_core(v)
+    near = z_turn(pair_up(v, swapped))
+    near2 = other_core(near)
+    return v, swapped, near, near2, far, other_core(far)
+
+
+def gather_heads_relay(v):
+    swapped = other_core(v)
+    near = z_turn(pair_up(v, swapped))
+    far = z_turn(near)
+    return v, swapped, near, other_core(near), far
+
+
 def memory_tail(attn, mem, w_out, proj):
-    pair = jnp.stack([attn, other_core(attn)])
-    four = jnp.concatenate([pair, z_near(pair)])
-    blocks = jnp.concatenate([four, z_far(four)])
+    blocks = gather_heads(attn)
     keep, send = memory_write(blocks, mem, w_out, proj)
     half = add(keep, other_core(send))
     half = add(half, z_near(half))
@@ -526,9 +613,7 @@
         x, in_hbm(memory), gain, *[in_hbm(w) for w in (w_query, w_key, w_value)]
     )
     weights = (gain, *weights)
-    q, kv1, w_out, mem_proj, cols = second_project(
-        x, *weights, q0, in_hbm(w_out.T), in_hbm(mem_proj)
-    )
+    q1, kv1, w_out, mem_proj, cols = second_project(x, *weights, in_hbm(w_out.T), in_hbm(mem_proj))
 
     part = memory_combine(part, x_near(part))
     part = memory_combine(part, x_far(part))
@@ -536,25 +621,26 @@
     attn = memory_combine(part, y_far(part), True)
     own, other = memory_tail(attn, memory, w_out, mem_proj)
 
-    kvs0 = [kv0] + [y_later(kv0, d) for d in (1, 2)]
-    kvs1 = [kv1] + [y_shift(kv1, d) for d in (1, 2, 3)]
+    next_row = y_later(kv0)
+    kvs0 = [kv0, next_row, y_later(next_row), next_row]
+    kvs1 = all_four(y_xor, kv1)
     qkvm1, part, mem1 = memory_project(own, other, *weights, kvs1)
     part = memory_combine(part, x_near(part))
     attn = memory_combine(part, x_far(part), True)
     own, other = memory_tail(attn, mem1, w_out, mem_proj)
 
-    hidden = None
-    qs = [q] + [x_shift(q, d) for d in (1, 2, 3)]
     for s, (kvs, qkvm) in enumerate(((kvs0, qkvm0), (kvs1, qkvm1))):
-        parts = token_attention(doc_ids, s, qs, kvs[2], kvs[1], kvs[0])
-        parts = [parts[0]] + [x_shift(parts[d], SHAPE - d) for d in (1, 2, 3)]
-        attn = token_combine(s, q, qkvm, parts)
-        blocks = []
-        for d in range(SHAPE):
-            piece = attn if d == 0 else z_shift(attn, d)
-            blocks += [piece, other_core(piece)]
-        hidden = token_out(blocks, cols, s, w_out, hidden)
-
+        own_q = (q0, q1)[s]
+        qs = all_four(x_xor, own_q)
+        parts = token_attention(doc_ids, s, qs, kvs[2], kvs[1], kvs[-1], kvs[0])
+        parts = [parts[0]] + [x_xor(parts[d], d) for d in (1, 2, 3)]
+        attn = token_combine(own_q, qkvm, parts)
+        blocks = gather_heads_relay(attn)
+        if s == 0:
+            hidden = token_out(blocks, cols, s, w_out)
+        else:
+            early = token_out_early(blocks[:4], cols, s, w_out)
+            hidden = token_out_late(blocks[4], early, s, w_out, hidden)
     return hidden.transpose(0, 2, 1), finish(own, other)
 
 

time: 167 us -> 160 us (0.958)
  waiting for transfers between devices: 55 us -> 49.5 us
  starting transfers between devices: 77.3 us -> 75.6 us
    ppermute x2, waiting for transfers between devices: 14 us -> 4.41 us  [x_near(): return lax.ppermute(v, 'seq', [(i, i ^ 1) for i in range(N_SEQ)])]
    ppermute x20 -> x25, starting transfers between devices: 28.4 us -> 36.1 us  [the longest x15 20.5 us: x_xor(): return lax.ppermute(v, 'seq', [(i, i ^ d) for i in range(N_SEQ)])]
    ppermute x4 -> x2, starting transfers between devices: 7.31 us -> 2.16 us  [z_far(): return lax.ppermute(v, 'head', [(i, i ^ 6) for i in range(N_HEAD)])]
    ppermute x20 -> x25, waiting for transfers between devices: 26.2 us -> 30.1 us  [the longest x6 13.8 us: z_turn(): lax.ppermute(v, 'head', [(i, (i + 2 - 4 * (i % 2)) % N_HEAD) for i in ran...]
    ppermute x14, starting transfers between devices: 27.6 us -> 24.3 us  [other_core(): return lax.ppermute(v, 'head', [(i, i ^ 1) for i in range(N_HEAD)])]
    pallas_call x2 -> x1, Pallas kernels: 3.68 us -> 1.83 us  [token_out(): pl.pallas_call(functools.partial(token_out_kernel, seg), grid=(1,), in_sp...]
    pallas_call x7 -> x13, Pallas kernels: 18.4 us -> 19.7 us  [the longest x2 7.13 us: token_attention(): pl.pallas_call(functools.partial(token_kernel, seg), in_specs=[WHOLE] * 9...]
    ppermute x4 -> x2, waiting for transfers between devices: 6.41 us -> 5.93 us  [z_near(): return lax.ppermute(v, 'head', [(i, i ^ 2) for i in range(N_HEAD)])]
  transfers between devices with their start and end apart: 48 -> 49, of which waited for: 20 -> 22; matrix products, arithmetic and copies ran while one was open for 0% -> 0% of each run, Pallas kernels for 14% -> 14%
where the time goes in v1:
time: 160 us; the launch traced here: 158 us
  starting transfers between devices  75.6 us (47%)
  waiting for transfers between devices  49.5 us (31%)
  Pallas kernels  30.9 us (19%)
    ppermute x14, starting transfers between devices, other_core(): return lax.ppermute(v, 'head', [(i, i ^ 1) for i in range(N_HEAD)])  24.3 us
    ppermute x15, starting transfers between devices, x_xor(): return lax.ppermute(v, 'seq', [(i, i ^ d) for i in range(N_SEQ)])  20.5 us
    ppermute x6, waiting for transfers between devices, z_turn(): lax.ppermute(v, 'head', [(i, (i + 2 - 4 * (i % 2)) % N_HEAD) for i in ran...  13.8 us
    ppermute x15, waiting for transfers between devices, x_xor(): return lax.ppermute(v, 'seq', [(i, i ^ d) for i in range(N_SEQ)])  11.9 us
    ppermute x6, starting transfers between devices, z_turn(): lax.ppermute(v, 'head', [(i, (i + 2 - 4 * (i % 2)) % N_HEAD) for i in ran...  7.68 us
    pallas_call x2, Pallas kernels, token_attention(): pl.pallas_call(functools.partial(token_kernel, seg), in_specs=[WHOLE] * 9...  7.13 us
    ppermute x2, starting transfers between devices, y_later(): lax.ppermute(v, 'seq', [(i, i + SHAPE) for i in range(N_SEQ - SHAPE)])  6.7 us
    ppermute x2, waiting for transfers between devices, z_near(): return lax.ppermute(v, 'head', [(i, i ^ 2) for i in range(N_HEAD)])  5.93 us
  transfers between devices with their start and end apart: 49, of which 22 were waited for; matrix products, arithmetic and copies ran while one was open for 0% of the time, Pallas kernels for 14%

profile of v1, /device:TPU:1, one launch (start us, length us, event | category | flops | bytes accessed | tf_op | source)
XLA Modules:
  0.0 157.8 jit_solution(16436644030660134706)
XLA Ops:
  1.3 5.1 %first_project.1 = (bf16[256,512]{1,0:T(8,128)(2,1)S(1)}, bf16[256,512]{1,0:T(8,128)(2,1)S(1)}, bf16[32,1024]{1,0:T(8,128)(2,1)S(1)}, bf16[64,384]{1,0:T(8,128)(...) custom-call(bf16[2,256,3584]{2,1,0:T(8,128)(2,1)} %x.3, ...), custom_call_target="tpu_custom_call" | custom-call | flops 2113929216 | bytes 10485760 | tf_op jit(solution)/shard_map/first_project/pallas_call | solution.py:147
  10.2 2.8 %collective-permute-start.1 = (bf16[64,384]{1,0:T(8,128)(2,1)S(1)}, bf16[64,384]{1,0:T(8,128)(2,1)S(1)}, u32[]{:S(2)}, u32[]{:S(2)}) collective-permute-start(bf16[64,384]{1,0:T(8,128)(2,1)S(1)} %memory_combine.6.a), channel_id=1, source_target_pairs={{0,24},{8,16},{16,8},{24,0},{32,56},{40,48},{48,40},{56,32},{64,88... | collective-permute-start | bytes 147464 | tf_op jit(solution)/shard_map/ppermute | solution.py:549
  17.9 3.0 %collective-permute-start.3 = (bf16[64,384]{1,0:T(8,128)(2,1)S(1)}, bf16[64,384]{1,0:T(8,128)(2,1)S(1)}, u32[]{:S(2)}, u32[]{:S(2)}) collective-permute-start(bf16[64,384]{1,0:T(8,128)(2,1)S(1)} %memory_combine.8.a), channel_id=1, source_target_pairs={{0,96},{8,104},{16,112},{24,120},{32,64},{40,72},{48,80},{56,88},{... | collective-permute-start | bytes 147464 | tf_op jit(solution)/shard_map/ppermute | solution.py:557
  22.6 5.2 %collective-permute-start.4 = (bf16[32,512]{1,0:T(8,128)(2,1)S(1)}, bf16[32,512]{1,0:T(8,128)(2,1)S(1)}, u32[]{:S(2)}, u32[]{:S(2)}) collective-permute-start(bf16[32,512]{1,0:T(8,128)(2,1)S(1)} %memory_combine.9.a.o), channel_id=1, source_target_pairs={{0,1},{1,0},{2,3},{3,2},{4,5},{5,4},{6,7},{7,6},{8,9},{9,8},{10,11... | collective-permute-start | bytes 98312 | tf_op jit(solution)/shard_map/ppermute | solution.py:577
  28.6 3.9 %collective-permute-start.5 = (bf16[2,32,512]{2,1,0:T(8,128)(2,1)S(1)}, bf16[2,32,512]{2,1,0:T(8,128)(2,1)S(1)}, u32[]{:S(2)}, u32[]{:S(2)}) collective-permute-start(bf16[2,32,512]{2,1,0:T(8,128)(2,1)S(1)} %pair_up.4), channel_id=1, source_target_pairs={{0,2},{1,7},{2,4},{3,1},{4,6},{5,3},{6,0},{7,5},{8,10},{9,15},{10,... | collective-permute-start | bytes 196616 | tf_op jit(solution)/shard_map/ppermute | solution.py:569
  32.5 4.4 %collective-permute-done.7.f = bf16[32,512]{1,0:T(8,128)(2,1)S(1)} collective-permute-done((bf16[32,512]{1,0:T(8,128)(2,1)S(1)}, bf16[32,512]{1,0:T(8,128)(2,1)S(1)}, u32[]{:S(2)}, u32[]{:S(2)}) %collective-permute-start.7) | collective-permute-done | bytes 32800 | tf_op jit(solution)/shard_map/ppermute | solution.py:573
  37.4 4.0 %second_project.1 = (bf16[256,512]{1,0:T(8,128)(2,1)S(1)}, bf16[256,512]{1,0:T(8,128)(2,1)S(1)}, bf16[448,4096]{1,0:T(8,128)(2,1)S(1)}, bf16[448,3584]{1,0:T(8,128)(2,1)S(1)}, bf16[2,256,512]{2,1,0:T(8,128)(2,1)S(1)}) custom-call(bf16[2,256,3584]{2,1,0:T(8,128)(2,1)} %x.3, bf16[3584]{0:T(1024)(128)(2,1)S(1)} %copy-done.1, ...), custom_call_target="tpu_custom_call" | custom-call | flops 1879048192 | bytes 10485760 | tf_op jit(solution)/shard_map/second_project/pallas_call | solution.py:206
  45.8 3.4 %collective-permute-done.10 = bf16[32,1792]{1,0:T(8,128)(2,1)S(1)} collective-permute-done((bf16[32,1792]{1,0:T(8,128)(2,1)S(1)}, bf16[32,1792]{1,0:T(8,128)(2,1)S(1)}, u32[]{:S(2)}, u32[]{:S(2)}) %collective-permute-start.10) | collective-permute-done | bytes 114720 | tf_op jit(solution)/shard_map/ppermute | solution.py:561
  50.9 2.7 %collective-permute-start.15 = (bf16[256,512]{1,0:T(8,128)(2,1)S(1)}, bf16[256,512]{1,0:T(8,128)(2,1)S(1)}, u32[]{:S(2)}, u32[]{:S(2)}) collective-permute-start(bf16[256,512]{1,0:T(8,128)(2,1)S(1)} %get-tuple-element.38.refs_0_.kvc), channel_id=1, source_target_pairs={{0,96},{8,104},{16,112},{24,120},{32,64},{40,72},{48,80},{56,88},{... | collective-permute-start | bytes 786440 | tf_op jit(solution)/shard_map/ppermute | solution.py:528
  58.7 2.5 %collective-permute-start.28 = (bf16[256,512]{1,0:T(8,128)(2,1)S(1)}, bf16[256,512]{1,0:T(8,128)(2,1)S(1)}, u32[]{:S(2)}, u32[]{:S(2)}) collective-permute-start(bf16[256,512]{1,0:T(8,128)(2,1)S(1)} %get-tuple-element.45.q0.q), channel_id=1, source_target_pairs={{0,24},{8,16},{16,8},{24,0},{32,56},{40,48},{48,40},{56,32},{64,88... | collective-permute-start | bytes 786440 | tf_op jit(solution)/shard_map/ppermute | solution.py:528
  64.5 5.4 %collective-permute-start.30 = (bf16[256,512]{1,0:T(8,128)(2,1)S(1)}, bf16[256,512]{1,0:T(8,128)(2,1)S(1)}, u32[]{:S(2)}, u32[]{:S(2)}) collective-permute-start(bf16[256,512]{1,0:T(8,128)(2,1)S(1)} %collective-permute-done.29.kvb.kvb2), channel_id=1, source_target_pairs={{0,32},{8,40},{16,48},{24,56},{32,64},{40,72},{48,80},{56,88},{64,... | collective-permute-start | bytes 786440 | tf_op jit(solution)/shard_map/ppermute | solution.py:536
  72.4 2.9 %collective-permute-done.38.b = bf16[64,384]{1,0:T(8,128)(2,1)S(1)} collective-permute-done((bf16[64,384]{1,0:T(8,128)(2,1)S(1)}, bf16[64,384]{1,0:T(8,128)(2,1)S(1)}, u32[]{:S(2)}, u32[]{:S(2)}) %collective-permute-start.38) | collective-permute-done | bytes 49184 | tf_op jit(solution)/shard_map/ppermute | solution.py:545
  75.5 2.6 %collective-permute-start.39 = (bf16[64,384]{1,0:T(8,128)(2,1)S(1)}, bf16[64,384]{1,0:T(8,128)(2,1)S(1)}, u32[]{:S(2)}, u32[]{:S(2)}) collective-permute-start(bf16[64,384]{1,0:T(8,128)(2,1)S(1)} %memory_combine.10.a), channel_id=1, source_target_pairs={{0,24},{8,16},{16,8},{24,0},{32,56},{40,48},{48,40},{56,32},{64,88... | collective-permute-start | bytes 147464 | tf_op jit(solution)/shard_map/ppermute | solution.py:549
  79.9 4.8 %collective-permute-start.40 = (bf16[32,512]{1,0:T(8,128)(2,1)S(1)}, bf16[32,512]{1,0:T(8,128)(2,1)S(1)}, u32[]{:S(2)}, u32[]{:S(2)}) collective-permute-start(bf16[32,512]{1,0:T(8,128)(2,1)S(1)} %memory_combine.11.a.o), channel_id=1, source_target_pairs={{0,1},{1,0},{2,3},{3,2},{4,5},{5,4},{6,7},{7,6},{8,9},{9,8},{10,11... | collective-permute-start | bytes 98312 | tf_op jit(solution)/shard_map/ppermute | solution.py:577
  91.2 3.6 %token_attention.3 = (bf16[272,512]{1,0:T(8,128)(2,1)S(1)}, bf16[272,512]{1,0:T(8,128)(2,1)S(1)}, bf16[272,512]{1,0:T(8,128)(2,1)S(1)}, bf16[272,512]{1,0:T(8,128)(2,1)S(1)}) custom-call(s32[2,4096]{1,0:T(2,128)S(1)} %copy-done.3, bf16[256,512]{1,0:T(8,128)(2,1)S(1)} %get-tuple-element.45.q0.q, bf16[256,512]{1,0:T(8,128)(2,1)S(1)} %collective-permute-done.26.q1, ...), custom_call_target="tpu_custom_call" | custom-call | flops 3000000000 | bytes 4000000 | tf_op jit(solution)/shard_map/token_attention/pallas_call | solution.py:402
  94.9 3.0 %collective-permute-start.32 = (bf16[272,512]{1,0:T(8,128)(2,1)S(1)}, bf16[272,512]{1,0:T(8,128)(2,1)S(1)}, u32[]{:S(2)}, u32[]{:S(2)}) collective-permute-start(bf16[272,512]{1,0:T(8,128)(2,1)S(1)} %get-tuple-element.50), channel_id=1, source_target_pairs={{0,16},{8,24},{16,0},{24,8},{32,48},{40,56},{48,32},{56,40},{64,80... | collective-permute-start | bytes 835592 | tf_op jit(solution)/shard_map/ppermute | solution.py:528
  103.1 3.6 %token_attention.2 = (bf16[272,512]{1,0:T(8,128)(2,1)S(1)}, bf16[272,512]{1,0:T(8,128)(2,1)S(1)}, bf16[272,512]{1,0:T(8,128)(2,1)S(1)}, bf16[272,512]{1,0:T(8,128)(2,1)S(1)}) custom-call(s32[2,4096]{1,0:T(2,128)S(1)} %copy-done.3, bf16[256,512]{1,0:T(8,128)(2,1)S(1)} %get-tuple-element.32.q0.q, bf16[256,512]{1,0:T(8,128)(2,1)S(1)} %collective-permute-done.16.q1, ...), custom_call_target="tpu_custom_call" | custom-call | flops 3000000000 | bytes 4000000 | tf_op jit(solution)/shard_map/token_attention/pallas_call | solution.py:402
  115.5 2.9 %collective-permute-start.34 = (bf16[256,512]{1,0:T(8,128)(2,1)S(1)}, bf16[256,512]{1,0:T(8,128)(2,1)S(1)}, u32[]{:S(2)}, u32[]{:S(2)}) collective-permute-start(bf16[256,512]{1,0:T(8,128)(2,1)S(1)} %token_combine.3.a.refs_0_), channel_id=1, source_target_pairs={{0,1},{1,0},{2,3},{3,2},{4,5},{5,4},{6,7},{7,6},{8,9},{9,8},{10,11... | collective-permute-start | bytes 786440 | tf_op jit(solution)/shard_map/ppermute | solution.py:577
  118.4 4.3 %collective-permute-done.20.c = bf16[272,512]{1,0:T(8,128)(2,1)S(1)} collective-permute-done((bf16[272,512]{1,0:T(8,128)(2,1)S(1)}, bf16[272,512]{1,0:T(8,128)(2,1)S(1)}, u32[]{:S(2)}, u32[]{:S(2)}) %collective-permute-start.20) | collective-permute-done | bytes 278560 | tf_op jit(solution)/shard_map/ppermute | solution.py:528
  122.7 3.1 %collective-permute-done.21.d = bf16[272,512]{1,0:T(8,128)(2,1)S(1)} collective-permute-done((bf16[272,512]{1,0:T(8,128)(2,1)S(1)}, bf16[272,512]{1,0:T(8,128)(2,1)S(1)}, u32[]{:S(2)}, u32[]{:S(2)}) %collective-permute-start.21) | collective-permute-done | bytes 278560 | tf_op jit(solution)/shard_map/ppermute | solution.py:528
  131.2 2.5 %collective-permute-done.46 = bf16[32,1792]{1,0:T(8,128)(2,1)S(1)} collective-permute-done((bf16[32,1792]{1,0:T(8,128)(2,1)S(1)}, bf16[32,1792]{1,0:T(8,128)(2,1)S(1)}, u32[]{:S(2)}, u32[]{:S(2)}) %collective-permute-start.46) | collective-permute-done | bytes 114720 | tf_op jit(solution)/shard_map/ppermute | solution.py:561
  134.3 5.5 %collective-permute-done.35.refs_2_ = bf16[2,256,512]{2,1,0:T(8,128)(2,1)S(1)} collective-permute-done((bf16[2,256,512]{2,1,0:T(8,128)(2,1)S(1)}, bf16[2,256,512]{2,1,0:T(8,128)(2,1)S(1)}, u32[]{:S(2)}, u32[]{:S(2)}) %collective-permute-start.35) | collective-permute-done | bytes 524320 | tf_op jit(solution)/shard_map/ppermute | solution.py:569
  141.2 4.2 %collective-permute-done.23.refs_2_ = bf16[2,256,512]{2,1,0:T(8,128)(2,1)S(1)} collective-permute-done((bf16[2,256,512]{2,1,0:T(8,128)(2,1)S(1)}, bf16[2,256,512]{2,1,0:T(8,128)(2,1)S(1)}, u32[]{:S(2)}, u32[]{:S(2)}) %collective-permute-start.23) | collective-permute-done | bytes 524320 | tf_op jit(solution)/shard_map/ppermute | solution.py:569
  153.8 2.9 %collective-permute-done.24.far = bf16[2,256,512]{2,1,0:T(8,128)(2,1)S(1)} collective-permute-done((bf16[2,256,512]{2,1,0:T(8,128)(2,1)S(1)}, bf16[2,256,512]{2,1,0:T(8,128)(2,1)S(1)}, u32[]{:S(2)}, u32[]{:S(2)}) %collective-permute-start.24) | collective-permute-done | bytes 524320 | tf_op jit(solution)/shard_map/ppermute | solution.py:569
  (111 shorter events, 68.7 us)
Async XLA Ops:
  54.9 9.6 %collective-permute-start.14 = (bf16[256,512]{1,0:T(8,128)(2,1)S(1)}, bf16[256,512]{1,0:T(8,128)(2,1)S(1)}, u32[]{:S(2)}, u32[]{:S(2)}) collective-permute-start(bf16[256,512]{1,0:T(8,128)(2,1)S(1)} %collective-permute-done.13.refs_1_.kvb), channel_id=1, source_target_pairs={{0,96},{8,104},{16,112},{24,120},{32,64},{40,72},{48,80},{56,88},{... | collective-permute-start | bytes 786440 | tf_op jit(solution)/shard_map/ppermute | solution.py:528
  55.7 14.2 %collective-permute-start.12 = (bf16[32,1792]{1,0:T(8,128)(2,1)S(1)}, bf16[32,1792]{1,0:T(8,128)(2,1)S(1)}, u32[]{:S(2)}, u32[]{:S(2)}) collective-permute-start(bf16[32,1792]{1,0:T(8,128)(2,1)S(1)} %add_convert_fusion.3.own), channel_id=1, source_target_pairs={{0,1},{1,0},{2,3},{3,2},{4,5},{5,4},{6,7},{7,6},{8,9},{9,8},{10,11... | collective-permute-start | bytes 344072 | tf_op jit(solution)/shard_map/ppermute | solution.py:577
  58.7 29.3 %collective-permute-start.28 = (bf16[256,512]{1,0:T(8,128)(2,1)S(1)}, bf16[256,512]{1,0:T(8,128)(2,1)S(1)}, u32[]{:S(2)}, u32[]{:S(2)}) collective-permute-start(bf16[256,512]{1,0:T(8,128)(2,1)S(1)} %get-tuple-element.45.q0.q), channel_id=1, source_target_pairs={{0,24},{8,16},{16,8},{24,0},{32,56},{40,48},{48,40},{56,32},{64,88... | collective-permute-start | bytes 786440 | tf_op jit(solution)/shard_map/ppermute | solution.py:528
  61.2 23.5 %collective-permute-start.16 = (bf16[256,512]{1,0:T(8,128)(2,1)S(1)}, bf16[256,512]{1,0:T(8,128)(2,1)S(1)}, u32[]{:S(2)}, u32[]{:S(2)}) collective-permute-start(bf16[256,512]{1,0:T(8,128)(2,1)S(1)} %get-tuple-element.32.q0.q), channel_id=1, source_target_pairs={{0,8},{8,0},{16,24},{24,16},{32,40},{40,32},{48,56},{56,48},{64,72... | collective-permute-start | bytes 786440 | tf_op jit(solution)/shard_map/ppermute | solution.py:528
  61.2 28.0 %collective-permute-start.27 = (bf16[256,512]{1,0:T(8,128)(2,1)S(1)}, bf16[256,512]{1,0:T(8,128)(2,1)S(1)}, u32[]{:S(2)}, u32[]{:S(2)}) collective-permute-start(bf16[256,512]{1,0:T(8,128)(2,1)S(1)} %collective-permute-done.26.q1), channel_id=1, source_target_pairs={{0,24},{8,16},{16,8},{24,0},{32,56},{40,48},{48,40},{56,32},{64,88... | collective-permute-start | bytes 786440 | tf_op jit(solution)/shard_map/ppermute | solution.py:528
  64.5 26.7 %collective-permute-start.30 = (bf16[256,512]{1,0:T(8,128)(2,1)S(1)}, bf16[256,512]{1,0:T(8,128)(2,1)S(1)}, u32[]{:S(2)}, u32[]{:S(2)}) collective-permute-start(bf16[256,512]{1,0:T(8,128)(2,1)S(1)} %collective-permute-done.29.kvb.kvb2), channel_id=1, source_target_pairs={{0,32},{8,40},{16,48},{24,56},{32,64},{40,72},{48,80},{56,88},{64,... | collective-permute-start | bytes 786440 | tf_op jit(solution)/shard_map/ppermute | solution.py:536
  84.7 10.1 %collective-permute-start.18 = (bf16[256,512]{1,0:T(8,128)(2,1)S(1)}, bf16[256,512]{1,0:T(8,128)(2,1)S(1)}, u32[]{:S(2)}, u32[]{:S(2)}) collective-permute-start(bf16[256,512]{1,0:T(8,128)(2,1)S(1)} %get-tuple-element.32.q0.q), channel_id=1, source_target_pairs={{0,24},{8,16},{16,8},{24,0},{32,56},{40,48},{48,40},{56,32},{64,88... | collective-permute-start | bytes 786440 | tf_op jit(solution)/shard_map/ppermute | solution.py:528
  87.2 12.1 %collective-permute-start.17 = (bf16[256,512]{1,0:T(8,128)(2,1)S(1)}, bf16[256,512]{1,0:T(8,128)(2,1)S(1)}, u32[]{:S(2)}, u32[]{:S(2)}) collective-permute-start(bf16[256,512]{1,0:T(8,128)(2,1)S(1)} %collective-permute-done.16.q1), channel_id=1, source_target_pairs={{0,24},{8,16},{16,8},{24,0},{32,56},{40,48},{48,40},{56,32},{64,88... | collective-permute-start | bytes 786440 | tf_op jit(solution)/shard_map/ppermute | solution.py:528
  88.1 13.7 %collective-permute-start.43 = (bf16[32,512]{1,0:T(8,128)(2,1)S(1)}, bf16[32,512]{1,0:T(8,128)(2,1)S(1)}, u32[]{:S(2)}, u32[]{:S(2)}) collective-permute-start(bf16[32,512]{1,0:T(8,128)(2,1)S(1)} %memory_combine.11.a.o), channel_id=1, source_target_pairs={{0,4},{1,5},{2,6},{3,7},{4,0},{5,1},{6,2},{7,3},{8,12},{9,13},{10,... | collective-permute-start | bytes 98312 | tf_op jit(solution)/shard_map/ppermute | solution.py:573
  89.3 13.8 %collective-permute-start.41 = (bf16[2,32,512]{2,1,0:T(8,128)(2,1)S(1)}, bf16[2,32,512]{2,1,0:T(8,128)(2,1)S(1)}, u32[]{:S(2)}, u32[]{:S(2)}) collective-permute-start(bf16[2,32,512]{2,1,0:T(8,128)(2,1)S(1)} %pair_up.7), channel_id=1, source_target_pairs={{0,2},{1,7},{2,4},{3,1},{4,6},{5,3},{6,0},{7,5},{8,10},{9,15},{10,... | collective-permute-start | bytes 196616 | tf_op jit(solution)/shard_map/ppermute | solution.py:569
  94.8 11.9 %collective-permute-start.31 = (bf16[272,512]{1,0:T(8,128)(2,1)S(1)}, bf16[272,512]{1,0:T(8,128)(2,1)S(1)}, u32[]{:S(2)}, u32[]{:S(2)}) collective-permute-start(bf16[272,512]{1,0:T(8,128)(2,1)S(1)} %get-tuple-element.49), channel_id=1, source_target_pairs={{0,8},{8,0},{16,24},{24,16},{32,40},{40,32},{48,56},{56,48},{64,72... | collective-permute-start | bytes 835592 | tf_op jit(solution)/shard_map/ppermute | solution.py:528
  94.9 17.9 %collective-permute-start.32 = (bf16[272,512]{1,0:T(8,128)(2,1)S(1)}, bf16[272,512]{1,0:T(8,128)(2,1)S(1)}, u32[]{:S(2)}, u32[]{:S(2)}) collective-permute-start(bf16[272,512]{1,0:T(8,128)(2,1)S(1)} %get-tuple-element.50), channel_id=1, source_target_pairs={{0,16},{8,24},{16,0},{24,8},{32,48},{40,56},{48,32},{56,40},{64,80... | collective-permute-start | bytes 835592 | tf_op jit(solution)/shard_map/ppermute | solution.py:528
  99.3 14.8 %collective-permute-start.33 = (bf16[272,512]{1,0:T(8,128)(2,1)S(1)}, bf16[272,512]{1,0:T(8,128)(2,1)S(1)}, u32[]{:S(2)}, u32[]{:S(2)}) collective-permute-start(bf16[272,512]{1,0:T(8,128)(2,1)S(1)} %get-tuple-element.51), channel_id=1, source_target_pairs={{0,24},{8,16},{16,8},{24,0},{32,56},{40,48},{48,40},{56,32},{64,88... | collective-permute-start | bytes 835592 | tf_op jit(solution)/shard_map/ppermute | solution.py:528
  106.7 11.7 %collective-permute-start.19 = (bf16[272,512]{1,0:T(8,128)(2,1)S(1)}, bf16[272,512]{1,0:T(8,128)(2,1)S(1)}, u32[]{:S(2)}, u32[]{:S(2)}) collective-permute-start(bf16[272,512]{1,0:T(8,128)(2,1)S(1)} %get-tuple-element.41), channel_id=1, source_target_pairs={{0,8},{8,0},{16,24},{24,16},{32,40},{40,32},{48,56},{56,48},{64,72... | collective-permute-start | bytes 835592 | tf_op jit(solution)/shard_map/ppermute | solution.py:528
  107.1 15.6 %collective-permute-start.20 = (bf16[272,512]{1,0:T(8,128)(2,1)S(1)}, bf16[272,512]{1,0:T(8,128)(2,1)S(1)}, u32[]{:S(2)}, u32[]{:S(2)}) collective-permute-start(bf16[272,512]{1,0:T(8,128)(2,1)S(1)} %get-tuple-element.42), channel_id=1, source_target_pairs={{0,16},{8,24},{16,0},{24,8},{32,48},{40,56},{48,32},{56,40},{64,80... | collective-permute-start | bytes 835592 | tf_op jit(solution)/shard_map/ppermute | solution.py:528
  108.4 17.3 %collective-permute-start.21 = (bf16[272,512]{1,0:T(8,128)(2,1)S(1)}, bf16[272,512]{1,0:T(8,128)(2,1)S(1)}, u32[]{:S(2)}, u32[]{:S(2)}) collective-permute-start(bf16[272,512]{1,0:T(8,128)(2,1)S(1)} %get-tuple-element.43), channel_id=1, source_target_pairs={{0,24},{8,16},{16,8},{24,0},{32,56},{40,48},{48,40},{56,32},{64,88... | collective-permute-start | bytes 835592 | tf_op jit(solution)/shard_map/ppermute | solution.py:528
  112.8 16.1 %collective-permute-start.45 = (bf16[32,1792]{1,0:T(8,128)(2,1)S(1)}, bf16[32,1792]{1,0:T(8,128)(2,1)S(1)}, u32[]{:S(2)}, u32[]{:S(2)}) collective-permute-start(bf16[32,1792]{1,0:T(8,128)(2,1)S(1)} %get-tuple-element.55), channel_id=1, source_target_pairs={{0,1},{1,0},{2,3},{3,2},{4,5},{5,4},{6,7},{7,6},{8,9},{9,8},{10,11... | collective-permute-start | bytes 344072 | tf_op jit(solution)/shard_map/ppermute | solution.py:577
  115.5 13.7 %collective-permute-start.34 = (bf16[256,512]{1,0:T(8,128)(2,1)S(1)}, bf16[256,512]{1,0:T(8,128)(2,1)S(1)}, u32[]{:S(2)}, u32[]{:S(2)}) collective-permute-start(bf16[256,512]{1,0:T(8,128)(2,1)S(1)} %token_combine.3.a.refs_0_), channel_id=1, source_target_pairs={{0,1},{1,0},{2,3},{3,2},{4,5},{5,4},{6,7},{7,6},{8,9},{9,8},{10,11... | collective-permute-start | bytes 786440 | tf_op jit(solution)/shard_map/ppermute | solution.py:577
  129.2 10.6 %collective-permute-start.35 = (bf16[2,256,512]{2,1,0:T(8,128)(2,1)S(1)}, bf16[2,256,512]{2,1,0:T(8,128)(2,1)S(1)}, u32[]{:S(2)}, u32[]{:S(2)}) collective-permute-start(bf16[2,256,512]{2,1,0:T(8,128)(2,1)S(1)} %pair_up.6), channel_id=1, source_target_pairs={{0,2},{1,7},{2,4},{3,1},{4,6},{5,3},{6,0},{7,5},{8,10},{9,15},{10,... | collective-permute-start | bytes 1572872 | tf_op jit(solution)/shard_map/ppermute | solution.py:569
  130.1 15.3 %collective-permute-start.23 = (bf16[2,256,512]{2,1,0:T(8,128)(2,1)S(1)}, bf16[2,256,512]{2,1,0:T(8,128)(2,1)S(1)}, u32[]{:S(2)}, u32[]{:S(2)}) collective-permute-start(bf16[2,256,512]{2,1,0:T(8,128)(2,1)S(1)} %pair_up.5), channel_id=1, source_target_pairs={{0,2},{1,7},{2,4},{3,1},{4,6},{5,3},{6,0},{7,5},{8,10},{9,15},{10,... | collective-permute-start | bytes 1572872 | tf_op jit(solution)/shard_map/ppermute | solution.py:569
  133.8 13.1 %collective-permute-start.47 = (bf16[32,1792]{1,0:T(8,128)(2,1)S(1)}, bf16[32,1792]{1,0:T(8,128)(2,1)S(1)}, u32[]{:S(2)}, u32[]{:S(2)}) collective-permute-start(bf16[32,1792]{1,0:T(8,128)(2,1)S(1)} %add_convert_fusion.1), channel_id=1, source_target_pairs={{0,6},{1,7},{2,4},{3,5},{4,2},{5,3},{6,0},{7,1},{8,14},{9,15},{10,... | collective-permute-start | bytes 344072 | tf_op jit(solution)/shard_map/ppermute | solution.py:565
  139.8 10.0 %collective-permute-start.36 = (bf16[2,256,512]{2,1,0:T(8,128)(2,1)S(1)}, bf16[2,256,512]{2,1,0:T(8,128)(2,1)S(1)}, u32[]{:S(2)}, u32[]{:S(2)}) collective-permute-start(bf16[2,256,512]{2,1,0:T(8,128)(2,1)S(1)} %collective-permute-done.35.refs_2_), channel_id=1, source_target_pairs={{0,1},{1,0},{2,3},{3,2},{4,5},{5,4},{6,7},{7,6},{8,9},{9,8},{10,11... | collective-permute-start | bytes 1572872 | tf_op jit(solution)/shard_map/ppermute | solution.py:577
  141.2 9.9 %collective-permute-start.37 = (bf16[2,256,512]{2,1,0:T(8,128)(2,1)S(1)}, bf16[2,256,512]{2,1,0:T(8,128)(2,1)S(1)}, u32[]{:S(2)}, u32[]{:S(2)}) collective-permute-start(bf16[2,256,512]{2,1,0:T(8,128)(2,1)S(1)} %collective-permute-done.35.refs_2_), channel_id=1, source_target_pairs={{0,2},{1,7},{2,4},{3,1},{4,6},{5,3},{6,0},{7,5},{8,10},{9,15},{10,... | collective-permute-start | bytes 1572872 | tf_op jit(solution)/shard_map/ppermute | solution.py:569
  146.8 9.9 %collective-permute-start.24 = (bf16[2,256,512]{2,1,0:T(8,128)(2,1)S(1)}, bf16[2,256,512]{2,1,0:T(8,128)(2,1)S(1)}, u32[]{:S(2)}, u32[]{:S(2)}) collective-permute-start(bf16[2,256,512]{2,1,0:T(8,128)(2,1)S(1)} %collective-permute-done.23.refs_2_), channel_id=1, source_target_pairs={{0,2},{1,7},{2,4},{3,1},{4,6},{5,3},{6,0},{7,5},{8,10},{9,15},{10,... | collective-permute-start | bytes 1572872 | tf_op jit(solution)/shard_map/ppermute | solution.py:569
  (29 other events, 193.6 us)
